TPU v7x, 256 devices: a whole 4x4x8 slice. The times are simulated.
256 devices in a mesh: bel: 64 (over z, x, y_lo), st: 4 (over y_hi, core).
Axes of the slice: x: 4, y: 4 (y_hi: 2, y_lo: 2; y = y_hi * 2 + y_lo), z: 8, core: 2. Of those that a mesh axis runs over, the one named last changes fastest.
Arguments:
- alphas: bfloat16 [512, 12288], P(None, 'st'), may hold values from -120 to 120
- transitions: bfloat16 [6, 12288, 12288], P(None, 'bel', 'st'), may hold values from 0.0009994507 to 10
- observe: bfloat16 [6, 48, 12288], P(None, None, 'st'), may hold values from 0.0019989014 to 0.19921875
- reward: bfloat16 [6, 12288], P(None, 'bel'), may hold values from -1.796875 to 1.796875
- belief_index: int32 [1024, 6, 48], P('bel'), may hold values from 0 to 511
- action: int32 [1024], replicated, may hold values from 0 to 5
Outputs:
- new_alphas: bfloat16 [1024, 12288], P('st', 'bel')
Inputs may be any that keep to these rules, and one draw needn't show every extreme that they name: `belief_index`: indices of rows of alphas.
All inputs are finite; a program needn't handle non-finite values.
Results may differ from a plain program's by a relative error of at most 0.0044.
Values may be sent and summed in bfloat16 or wider, within the bound.
No kernel may reach another device: no remote copies, remote signals or barrier semaphores. Data moves between devices by JAX's collectives and lax.ppermute only.
A program may use at most 128 MiB of HBM per device.

v0:
```python
import math

import jax
import jax.numpy as jnp
from jax import lax
from jax.sharding import Mesh
from jax.sharding import PartitionSpec as P

S = 12288
ACTS = 6
BEL = ("bel_0", "bel_1", "bel_2")


discount = 0.95


def laid_out(blocks, dim):
    dims = list(blocks.shape[1:])
    dims[dim] *= blocks.shape[0]
    return jnp.moveaxis(blocks, 0, dim).reshape(dims)


def stacked_from(value, axes, sequence):
    blocks = value
    for k in sequence:
        blocks = lax.all_gather(blocks, axes[k])
    done = sequence[::-1]
    back = [done.index(k) for k in range(len(axes))]
    blocks = blocks.transpose(*back, *range(len(axes), blocks.ndim))
    return blocks.reshape(-1, *value.shape)


def gather_axes(value, axes, sequence, dim):
    return laid_out(stacked_from(value, axes, sequence), dim)


def in_blocks(value, dim, peers):
    dims = value.shape
    blocks = value.reshape(*dims[:dim], peers, dims[dim] // peers, *dims[dim + 1 :])
    return jnp.moveaxis(blocks, dim, 0)


def sum_at_owner(value, axis, dim):
    peers = lax.axis_size(axis)
    blocks = lax.all_to_all(in_blocks(value, dim, peers), axis, 0, 0, tiled=True)
    return jnp.sum(blocks, axis=0)


def mixture_block(alphas, observe, index_rows, action_rows):
    onehot = action_rows[:, None] == jnp.arange(ACTS, dtype=jnp.int32)[None, :]
    chosen = jnp.sum(jnp.where(onehot[:, :, None], index_rows, 0), axis=1)
    picked = alphas[chosen]
    weights = observe[action_rows]
    mixed = jnp.einsum("bos,bos->bs", picked, weights, preferred_element_type=jnp.float32)
    return mixed.astype(jnp.bfloat16)


def grouped_product(rows, acts, weights, block):
    count = rows.shape[0]
    kinds = weights.shape[0]
    blocks = count // block + kinds - 1
    onehot = (acts[:, None] == jnp.arange(kinds, dtype=jnp.int32)[None, :]).astype(jnp.int32)
    totals = jnp.sum(onehot, axis=0)
    filled = (totals + block - 1) // block
    ends = jnp.cumsum(filled)
    starts = ends - filled
    before = jnp.cumsum(onehot, axis=0) - onehot
    rank = jnp.sum(before * onehot, axis=1)
    first = jnp.sum(onehot * starts[None, :], axis=1)
    target = first * block + rank
    source = (
        jnp.zeros((blocks * block,), jnp.int32).at[target].set(jnp.arange(count, dtype=jnp.int32))
    )
    padded = rows[source].reshape(blocks, block, rows.shape[1])
    owner = jnp.sum(
        (jnp.arange(blocks, dtype=jnp.int32)[:, None] >= ends[None, :]).astype(jnp.int32), axis=1
    )
    owner = jnp.minimum(owner, kinds - 1)

    def one_block(pair):
        part, which = pair
        matrix = lax.dynamic_index_in_dim(weights, which, 0, keepdims=False)
        return lax.dot_general(
            part, matrix, (((1,), (1,)), ((), ())), preferred_element_type=jnp.float32
        )

    result = lax.map(one_block, (padded, owner)).reshape(blocks * block, weights.shape[1])
    return result[target]


def body(alphas, transitions, observe, reward, belief_index, action):
    bel_rows = belief_index.shape[0]
    beliefs = action.shape[0]
    own_start = lax.axis_index(BEL) * bel_rows
    own_action = lax.dynamic_slice_in_dim(action, own_start, bel_rows)
    mixture = mixture_block(alphas, observe, belief_index, own_action)
    gathered = gather_axes(mixture, BEL, (2, 0, 1), 0)
    terms = grouped_product(gathered, action, transitions, math.gcd(beliefs, 256))
    summed = sum_at_owner(terms, "st", 0)
    out_rows = summed.shape[0]
    row_action = lax.dynamic_slice_in_dim(action, lax.axis_index("st") * out_rows, out_rows)
    onehot = (row_action[:, None] == jnp.arange(ACTS, dtype=jnp.int32)[None, :]).astype(
        jnp.bfloat16
    )
    gained = jnp.dot(onehot, reward, preferred_element_type=jnp.float32)
    return (gained + discount / S * summed).astype(jnp.bfloat16)


def solution(mesh):
    torus = Mesh(mesh.devices.reshape(8, 4, 2, mesh.shape["st"]), ("bel_0", "bel_1", "bel_2", "st"))
    in_specs = (
        P(None, "st"),
        P(None, BEL, "st"),
        P(None, None, "st"),
        P(None, BEL),
        P(BEL, None, None),
        P(),
    )
    out_specs = P("st", BEL)
    return jax.shard_map(body, mesh=torus, in_specs=in_specs, out_specs=out_specs, check_vma=False)
```

profile of v0, /device:TPU:1, one launch (start us, length us, event | category | flops | bytes accessed | tf_op | source)
XLA Modules:
  0.0 265.4 jit_solution(5997276826388490618)
XLA Ops:
  6.5 0.9 compare_select_fusion.3
  7.5 0.9 select_reduce_fusion
  8.5 5.0 %gather_fusion = bf16[768,3072]{1,0:T(8,128)(2,1)} fusion(bf16[512,3072]{1,0:T(8,128)(2,1)S(1)} %copy-done, s32[1024]{0:T(1024)S(1)} %pad_clamp_fusion.2), kind=kCustom, calls=%fused_computation | custom fusion | bytes 9440256 | tf_op jit(solution)/shard_map/gather | solution.py:52
  13.5 4.5 %gather_fusion.1 = bf16[16,48,3072]{2,1,0:T(8,128)(2,1)} fusion(bf16[6,48,3072]{2,1,0:T(8,128)(2,1)} %param.10, s32[1024]{0:T(1024)S(1)} %pad_clamp_fusion.1), kind=kCustom, calls=%fused_computation.1 | custom fusion | bytes 9437248 | tf_op jit(solution)/shard_map/gather | solution.py:53
  18.0 5.7 %fusion.16 = bf16[16,3072]{1,0:T(8,128)(2,1)S(1)} fusion(bf16[16,3072,48]{1,2,0:T(8,128)(2,1)} %bitcast.73, bf16[16,48,3072]{2,1,0:T(8,128)(2,1)} %gather_fusion.1), kind=kLoop, calls=%fused_computation.14 | loop fusion | flops 9388032 | bytes 9535488 | tf_op jit(solution)/shard_map/bos,bos->bs/dot_general | solution.py:54
  23.7 4.9 %all-gather = bf16[32,3072]{1,0:T(8,128)(2,1)} all-gather(bf16[16,3072]{1,0:T(8,128)(2,1)S(1)} %fusion.16), channel_id=2, replica_groups=mesh['bel_0'=8,'bel_1'=4,'bel_2'=2,'st'=4] {'bel_2'}, dimensions={0}, use_global_device_ids=true | all-gather | bytes 294912 | tf_op jit(solution)/shard_map/all_gather | solution.py:26
  28.7 40.1 %all-gather.6.cloned.1.call-done = bf16[16,16,3072]{2,1,0:T(8,128)(2,1)} async-done(((bf16[2,16,3072]{2,1,0:T(8,128)(2,1)}), bf16[16,16,3072]{2,1,0:T(8,128)(2,1)}) %all-gather.6.cloned.1.call-update) | async-done | bytes 1572880 | tf_op jit(solution)/shard_map/all_gather | solution.py:26
  69.2 1.7 reduce-window.18
  71.5 4.3 %scatter_custom_fusion = s32[2304]{0:T(1024)S(1)} fusion(s32[1024]{0:T(1024)S(1)} %bitcast.80, s32[1024]{0:T(1024)S(1)} %iota.22, s32[]{:T(128)} %constant.41.clone.1), kind=kCustom, calls=%fused_computation.35 | custom fusion | bytes 9220 | tf_op jit(solution)/shard_map/scatter | solution.py:72
  75.9 65.1 %all-gather.8.cloned.1.call-done = bf16[32,2,16,3072]{3,2,1,0:T(8,128)(2,1)} async-done(((bf16[8,2,16,3072]{3,2,1,0:T(8,128)(2,1)}), bf16[32,2,16,3072]{3,2,1,0:T(8,128)(2,1)}) %all-gather.8.cloned.1.call-update) | async-done | bytes 6291472 | tf_op jit(solution)/shard_map/all_gather | solution.py:26
  141.1 6.2 %copy.15 = bf16[8,4,2,16,3072]{4,3,2,1,0:T(8,128)(2,1)} copy(bf16[8,4,2,16,3072]{4,3,2,0,1:T(8,128)(2,1)} %bitcast.74) | data formatting | bytes 12582912 | tf_op jit(solution)/shard_map/transpose | solution.py:29
  147.3 29.4 %gather_fusion.2 = bf16[2304,3072]{1,0:T(8,128)(2,1)} fusion(bf16[1024,3072]{1,0:T(8,128)(2,1)} %bitcast.70, s32[3072]{0:T(1024)S(1)} %pad_clamp_fusion), kind=kCustom, calls=%fused_computation.2 | custom fusion | bytes 28320768 | tf_op jit(solution)/shard_map/gather | solution.py:74
  176.7 50.6 %while.10 = (s32[]{:T(128)}, f32[9,256,192]{1,2,0:T(8,128)}, bf16[9,256,3072]{2,1,0:T(8,128)(2,1)}, s32[9]{0:T(128)S(1)}, bf16[6,192,3072]{2,1,0:T(8,128)(2,1)}, /*index=5*/s32[]{:T(128)}, s32[]{:T(128)}, s32[]{:T(128)}) while((s32[]{:T(128)}, f32[9,256,192]{1,2,0:T(8,128)}, bf16[9,256,3072]{2,1,0:T(8,128)(2,1)}, s32[9]{0:T(128)S(1)}, ...), condition=%wide.region_10.11_spmd, body=%wide.region_9.10_spmd.sunk | while | flops 301989888 | bytes 2950279 | solution.py:87
  176.7 0.6 dynamic_slice.42
  179.2 3.1 %fusion.31 = f32[9,256,192]{1,2,0:T(8,128)} fusion(f32[9,256,192]{1,2,0:T(8,128)} %get-tuple-element.87, s32[]{:T(128)} %get-tuple-element.86, bf16[6,192,3072]{2,1,0:T(8,128)(2,1)} %get-tuple-element.98, s32[]{:T(128)S(6)} %select_n.78, bf16[9,256,3072]{2,1,0:T(8,128)(2,1)} %get-tuple-element.96), kind=kOutput, calls=%fused_computation.11.clone.1 | convolution fusion | flops 301989888 | bytes 2950148 | tf_op jit(solution)/shard_map/while/body/eval_jaxpr/dot_general | solution.py:83
  182.3 0.6 dynamic_slice.42
  184.8 3.1 %fusion.31 = f32[9,256,192]{1,2,0:T(8,128)} fusion(f32[9,256,192]{1,2,0:T(8,128)} %get-tuple-element.87, s32[]{:T(128)} %get-tuple-element.86, bf16[6,192,3072]{2,1,0:T(8,128)(2,1)} %get-tuple-element.98, s32[]{:T(128)S(6)} %select_n.78, bf16[9,256,3072]{2,1,0:T(8,128)(2,1)} %get-tuple-element.96), kind=kOutput, calls=%fused_computation.11.clone.1 | convolution fusion | flops 301989888 | bytes 2950148 | tf_op jit(solution)/shard_map/while/body/eval_jaxpr/dot_general | solution.py:83
  187.9 0.6 dynamic_slice.42
  190.4 3.1 %fusion.31 = f32[9,256,192]{1,2,0:T(8,128)} fusion(f32[9,256,192]{1,2,0:T(8,128)} %get-tuple-element.87, s32[]{:T(128)} %get-tuple-element.86, bf16[6,192,3072]{2,1,0:T(8,128)(2,1)} %get-tuple-element.98, s32[]{:T(128)S(6)} %select_n.78, bf16[9,256,3072]{2,1,0:T(8,128)(2,1)} %get-tuple-element.96), kind=kOutput, calls=%fused_computation.11.clone.1 | convolution fusion | flops 301989888 | bytes 2950148 | tf_op jit(solution)/shard_map/while/body/eval_jaxpr/dot_general | solution.py:83
  196.1 3.1 %fusion.31 = f32[9,256,192]{1,2,0:T(8,128)} fusion(f32[9,256,192]{1,2,0:T(8,128)} %get-tuple-element.87, s32[]{:T(128)} %get-tuple-element.86, bf16[6,192,3072]{2,1,0:T(8,128)(2,1)} %get-tuple-element.98, s32[]{:T(128)S(6)} %select_n.78, bf16[9,256,3072]{2,1,0:T(8,128)(2,1)} %get-tuple-element.96), kind=kOutput, calls=%fused_computation.11.clone.1 | convolution fusion | flops 301989888 | bytes 2950148 | tf_op jit(solution)/shard_map/while/body/eval_jaxpr/dot_general | solution.py:83
  201.7 3.1 %fusion.31 = f32[9,256,192]{1,2,0:T(8,128)} fusion(f32[9,256,192]{1,2,0:T(8,128)} %get-tuple-element.87, s32[]{:T(128)} %get-tuple-element.86, bf16[6,192,3072]{2,1,0:T(8,128)(2,1)} %get-tuple-element.98, s32[]{:T(128)S(6)} %select_n.78, bf16[9,256,3072]{2,1,0:T(8,128)(2,1)} %get-tuple-element.96), kind=kOutput, calls=%fused_computation.11.clone.1 | convolution fusion | flops 301989888 | bytes 2950148 | tf_op jit(solution)/shard_map/while/body/eval_jaxpr/dot_general | solution.py:83
  207.3 3.1 %fusion.31 = f32[9,256,192]{1,2,0:T(8,128)} fusion(f32[9,256,192]{1,2,0:T(8,128)} %get-tuple-element.87, s32[]{:T(128)} %get-tuple-element.86, bf16[6,192,3072]{2,1,0:T(8,128)(2,1)} %get-tuple-element.98, s32[]{:T(128)S(6)} %select_n.78, bf16[9,256,3072]{2,1,0:T(8,128)(2,1)} %get-tuple-element.96), kind=kOutput, calls=%fused_computation.11.clone.1 | convolution fusion | flops 301989888 | bytes 2950148 | tf_op jit(solution)/shard_map/while/body/eval_jaxpr/dot_general | solution.py:83
  212.9 3.1 %fusion.31 = f32[9,256,192]{1,2,0:T(8,128)} fusion(f32[9,256,192]{1,2,0:T(8,128)} %get-tuple-element.87, s32[]{:T(128)} %get-tuple-element.86, bf16[6,192,3072]{2,1,0:T(8,128)(2,1)} %get-tuple-element.98, s32[]{:T(128)S(6)} %select_n.78, bf16[9,256,3072]{2,1,0:T(8,128)(2,1)} %get-tuple-element.96), kind=kOutput, calls=%fused_computation.11.clone.1 | convolution fusion | flops 301989888 | bytes 2950148 | tf_op jit(solution)/shard_map/while/body/eval_jaxpr/dot_general | solution.py:83
  218.6 3.1 %fusion.31 = f32[9,256,192]{1,2,0:T(8,128)} fusion(f32[9,256,192]{1,2,0:T(8,128)} %get-tuple-element.87, s32[]{:T(128)} %get-tuple-element.86, bf16[6,192,3072]{2,1,0:T(8,128)(2,1)} %get-tuple-element.98, s32[]{:T(128)S(6)} %select_n.78, bf16[9,256,3072]{2,1,0:T(8,128)(2,1)} %get-tuple-element.96), kind=kOutput, calls=%fused_computation.11.clone.1 | convolution fusion | flops 301989888 | bytes 2950148 | tf_op jit(solution)/shard_map/while/body/eval_jaxpr/dot_general | solution.py:83
  224.2 3.1 %fusion.31 = f32[9,256,192]{1,2,0:T(8,128)} fusion(f32[9,256,192]{1,2,0:T(8,128)} %get-tuple-element.87, s32[]{:T(128)} %get-tuple-element.86, bf16[6,192,3072]{2,1,0:T(8,128)(2,1)} %get-tuple-element.98, s32[]{:T(128)S(6)} %select_n.78, bf16[9,256,3072]{2,1,0:T(8,128)(2,1)} %get-tuple-element.96), kind=kOutput, calls=%fused_computation.11.clone.1 | convolution fusion | flops 301989888 | bytes 2950148 | tf_op jit(solution)/shard_map/while/body/eval_jaxpr/dot_general | solution.py:83
  227.3 3.0 %copy.16 = f32[9,256,192]{2,1,0:T(8,128)} copy(f32[9,256,192]{1,2,0:T(8,128)} %get-tuple-element.32) | data formatting | bytes 3538944 | tf_op jit(solution)/shard_map/while | solution.py:87
  230.3 6.3 %gather_fusion.3 = f32[1024,192]{1,0:T(8,128)} fusion(f32[2304,192]{1,0:T(8,128)} %bitcast.71, s32[1024]{0:T(1024)S(1)} %broadcast_clamp_fusion), kind=kCustom, calls=%fused_computation.3 | custom fusion | bytes 1576960 | tf_op jit(solution)/shard_map/gather | solution.py:88
  236.6 2.4 copy.17
  239.0 5.1 %all-to-all-start = ((f32[4,256,192]{1,2,0:T(8,128)}), f32[4,256,192]{1,2,0:T(8,128)}, u32[]{:S(2)}, u32[]{:S(2)}) async-start(f32[4,256,192]{1,2,0:T(8,128)} %copy.17), calls=%async_computation | async-start | bytes 1572864 | tf_op jit(solution)/shard_map/all_to_all | solution.py:45
  244.2 12.2 %all-to-all-done = f32[4,256,192]{1,2,0:T(8,128)} async-done(((f32[4,256,192]{1,2,0:T(8,128)}), f32[4,256,192]{1,2,0:T(8,128)}, u32[]{:S(2)}, u32[]{:S(2)}) %all-to-all-start) | async-done | bytes 786464 | tf_op jit(solution)/shard_map/all_to_all | solution.py:45
  256.4 1.2 reduce_sum.62
  257.6 0.9 fusion.17
  (40 shorter events, 4.9 us)
Async XLA Ops:
  6.5 2.0 copy-start
  6.5 62.3 %all-gather.6.cloned.1.call-start = ((), (), s32[]{:S(2)}) async-start(), calls=%async_computation.1 | async-start | bytes 1769472 | tf_op jit(solution)/shard_map/all_gather | solution.py:26
  18.0 50.9 %copy-start.1 = (s32[1024]{0:T(1024)S(1)}, s32[1024]{0:T(1024)}, u32[]{:S(2)}) copy-start(s32[1024]{0:T(1024)} %param.13) | copy-start | bytes 12292
  28.6 112.5 %all-gather.8.cloned.1.call-start = ((), (), s32[]{:S(2)}) async-start(), calls=%async_computation.2 | async-start | bytes 7864320 | tf_op jit(solution)/shard_map/all_gather | solution.py:26
  230.3 27.3 %copy-start.2 = (bf16[6,192]{1,0:T(8,128)(2,1)S(1)}, bf16[6,192]{1,0:T(8,128)(2,1)}, u32[]{:S(2)}) copy-start(bf16[6,192]{1,0:T(8,128)(2,1)} %param.11) | copy-start | bytes 6916
  239.0 17.4 %all-to-all-start = ((f32[4,256,192]{1,2,0:T(8,128)}), f32[4,256,192]{1,2,0:T(8,128)}, u32[]{:S(2)}, u32[]{:S(2)}) async-start(f32[4,256,192]{1,2,0:T(8,128)} %copy.17), calls=%async_computation | async-start | bytes 1572864 | tf_op jit(solution)/shard_map/all_to_all | solution.py:45
Sparse Core Ops, SparseCore 0:
  28.7 40.0 all-gather.5
  70.6 70.4 all-gather.7
where the time goes:
time: 266 us; the launch traced here: 265 us
  waiting for transfers between devices  117 us (44%)
  local copies, waits for them, and re-layouts  67 us (25%)
  matrix products  28.9 us (11%)
  loops' own time  17.2 us (6%)
  between operations  13.5 us (5%)
  other arithmetic  11.3 us (4%)
  starting transfers between devices  5.16 us (2%)
  blocking collectives  4.88 us (2%)
    all_gather x2, waiting for transfers between devices, stacked_from(): blocks = lax.all_gather(blocks, axes[k])  105 us
    gather x1, local copies, waits for them, and re-layouts, grouped_product(): padded = rows[source].reshape(blocks, block, rows.shape[1])  29.4 us
    dot_general x9, matrix products, one_block(): lax.dot_general(part, matrix, (((1,), (1,)), ((), ())), preferred_element...  28 us
    another operation x1, loops' own time, grouped_product(): lax.map(one_block, (padded, owner))  17.2 us
    all_to_all x1, waiting for transfers between devices, sum_at_owner(): lax.all_to_all(in_blocks(value, dim, peers), axis, 0, 0, tiled=True)  12.2 us
    gather x1, local copies, waits for them, and re-layouts, grouped_product(): return result[target]  6.33 us
    transpose x1, local copies, waits for them, and re-layouts, stacked_from(): blocks = blocks.transpose(*back, *range(len(axes), blocks.ndim))  6.17 us
    dot_general x1, other arithmetic, mixture_block(): jnp.einsum('bos,bos->bs', picked, weights, preferred_element_type=jnp.flo...  5.75 us
  transfers between devices with their start and end apart: 3, of which 3 were waited for; matrix products, arithmetic and copies ran while one was open for 3% of the time, Pallas kernels for 0%

commit v1 on v0

v1 whole, which is shorter than its diff:
```python
import functools

import jax
import jax.numpy as jnp
from jax import lax
from jax.experimental import pallas as pl
from jax.experimental.pallas import tpu as pltpu
from jax.sharding import Mesh
from jax.sharding import PartitionSpec as P

S = 12288
ACTS = 6
OBS = 48
ALPHAS = 512
BELIEFS = 1024
BEL = ("z", "x", "yl")
PEERS = 64
OWN = BELIEFS // PEERS
COLS = 3072
ROWS = 192
SUB = COLS // 128
CHUNK = 256
STEPS = BELIEFS // CHUNK
DISCOUNT = 0.95

NT = (((1,), (1,)), ((), ()))
NN = (((1,), (0,)), ((), ()))


def order_kernel(action_ref, index_ref, table_ref, sorted_ref, target_ref):
    act = action_ref[...]
    member = (lax.broadcasted_iota(jnp.int32, (8, BELIEFS), 0) == act).astype(jnp.float32)
    earlier = (
        lax.broadcasted_iota(jnp.int32, (BELIEFS, BELIEFS), 0)
        < lax.broadcasted_iota(jnp.int32, (BELIEFS, BELIEFS), 1)
    ).astype(jnp.float32).astype(jnp.bfloat16)
    before = lax.dot_general(member.astype(jnp.bfloat16), earlier, NN, preferred_element_type=jnp.float32)
    totals = jnp.sum(member, axis=1, keepdims=True)
    position = lax.broadcasted_iota(jnp.int32, (1, BELIEFS), 1)
    start = jnp.zeros((1, 1), jnp.float32)
    target = jnp.zeros((1, BELIEFS), jnp.float32)
    owner = jnp.zeros((1, BELIEFS), jnp.int32)
    for a in range(ACTS):
        target = target + member[a : a + 1] * (before[a : a + 1] + start)
        start = start + totals[a : a + 1]
        if a < ACTS - 1:
            owner = owner + (position >= start.astype(jnp.int32)).astype(jnp.int32)
    target = target.astype(jnp.int32)
    target_ref[...] = target
    sorted_ref[...] = owner
    index = index_ref[...]
    parts = jnp.concatenate([index >> 4, index & 15], axis=0).astype(jnp.float32).astype(jnp.bfloat16)
    for c in range(BELIEFS // 256):
        moved = (
            lax.broadcasted_iota(jnp.int32, (256, BELIEFS), 0) + c * 256 == target
        ).astype(jnp.float32).astype(jnp.bfloat16)
        got = lax.dot_general(parts, moved, NT, preferred_element_type=jnp.float32).astype(jnp.int32)
        table_ref[:, c * 256 : (c + 1) * 256] = (got[:OBS] * 16 + got[OBS:]) * SUB


def main_kernel(
    core_ref, table_ref, sorted_ref, owner_ref, target_ref, alphas_ref, observe_ref, weights_ref,
    keep_ref, send_ref, rows_ref, obs_ref, mix_ref, block_ref, terms_ref,
):
    step = pl.program_id(0)

    @pl.when(step == 0)
    def _():
        def spread(source, dest):
            def body(k, _):
                for j in range(SUB):
                    part = source[pl.ds(pl.multiple_of(k * 16, 16), 16), j * 128 : (j + 1) * 128]
                    dest[pl.ds(k * 16 * SUB + j, 16, stride=SUB), :] = part.astype(jnp.float32)
                return 0

            lax.fori_loop(0, source.shape[0] // 16, body, 0)

        spread(alphas_ref, rows_ref)
        spread(observe_ref, obs_ref)

    base = step * CHUNK

    def row(at):
        return rows_ref[pl.ds(pl.multiple_of(at, 8), SUB), :]

    def weight(at):
        return obs_ref[pl.ds(pl.multiple_of(at, 8), SUB), :]

    def sixteen(i, _):
        for half in range(2):
            first = i * 16 + half * 8
            a0 = sorted_ref[0, base + first]
            a1 = sorted_ref[0, base + first + 7]

            @pl.when(a0 == a1)
            def _():
                sums = [None] * 8
                for o in range(OBS):
                    w = weight((a0 * OBS + o) * SUB)
                    for r in range(8):
                        term = row(table_ref[o, first + r]) * w
                        sums[r] = term if o == 0 else sums[r] + term
                for r in range(8):
                    mix_ref[(half * 8 + r) * SUB : (half * 8 + r + 1) * SUB, :] = sums[r]

            @pl.when(a0 != a1)
            def _():
                def one(r, _):
                    a = sorted_ref[0, base + first + r]
                    total = None
                    for o in range(OBS):
                        term = row(table_ref[o, first + r]) * weight((a * OBS + o) * SUB)
                        total = term if o == 0 else total + term
                    mix_ref[pl.ds(pl.multiple_of((half * 8 + r) * SUB, 8), SUB), :] = total
                    return 0

                lax.fori_loop(0, 8, one, 0)

        for j in range(SUB):
            part = mix_ref[pl.ds(j, 16, stride=SUB), :]
            block_ref[pl.ds(pl.multiple_of(i * 16, 16), 16), j * 128 : (j + 1) * 128] = part.astype(jnp.bfloat16)
        return 0

    lax.fori_loop(0, CHUNK // 16, sixteen, 0)

    low = sorted_ref[0, base]
    high = sorted_ref[0, base + CHUNK - 1]
    here = pl.ds(pl.multiple_of(base, 128), CHUNK)
    owner = owner_ref[:, here]

    def three(t, _):
        a = jnp.minimum(low + 3 * t, ACTS - 3)
        matrix = weights_ref[pl.ds(pl.multiple_of(a * ROWS, 64), 3 * ROWS), :]
        got = lax.dot_general(matrix, block_ref[...], NT, preferred_element_type=jnp.float32)
        value = terms_ref[:, here]
        for d in range(3):
            value = jnp.where(owner == a + d, got[d * ROWS : (d + 1) * ROWS], value)
        terms_ref[:, here] = value
        return 0

    lax.fori_loop(0, (high - low) // 3 + 1, three, 0)

    @pl.when(step == STEPS - 1)
    def _():
        terms = terms_ref[...]
        big = terms.astype(jnp.bfloat16)
        small = (terms - big.astype(jnp.float32)).astype(jnp.bfloat16)
        both = jnp.concatenate([big, small], axis=0)
        core = core_ref[0]
        for ref, side in ((keep_ref, core), (send_ref, 1 - core)):
            for yh in range(2):
                at = pl.multiple_of((2 * yh + side) * 256, 128)
                moved = (
                    lax.broadcasted_iota(jnp.int32, (BELIEFS, 256), 0) == target_ref[:, pl.ds(at, 256)]
                ).astype(jnp.float32).astype(jnp.bfloat16)
                got = lax.dot_general(both, moved, NN, preferred_element_type=jnp.float32)
                ref[:, yh * 256 : (yh + 1) * 256] = got[:ROWS] + got[ROWS:]


def vmem():
    return pl.BlockSpec(memory_space=pltpu.VMEM)


def smem():
    return pl.BlockSpec(memory_space=pltpu.SMEM)


def body(alphas, transitions, observe, reward, belief_index, action):
    bel = lax.axis_index(BEL)
    core = lax.axis_index("co")
    high = lax.axis_index("yh")
    own_action = lax.dynamic_slice_in_dim(action, bel * OWN, OWN)
    onehot = own_action[:, None] == jnp.arange(ACTS, dtype=jnp.int32)[None, :]
    chosen = jnp.sum(jnp.where(onehot[:, :, None], belief_index, 0), axis=1)
    spread = jnp.broadcast_to(chosen[None], (PEERS, OWN, OBS))
    index = lax.all_to_all(spread, BEL, 0, 0, tiled=True)
    index = index.reshape(BELIEFS, OBS).T
    table, owner, target = pl.pallas_call(
        order_kernel,
        out_shape=(
            jax.ShapeDtypeStruct((OBS, BELIEFS), jnp.int32),
            jax.ShapeDtypeStruct((1, BELIEFS), jnp.int32),
            jax.ShapeDtypeStruct((1, BELIEFS), jnp.int32),
        ),
        in_specs=[vmem(), vmem()],
        out_specs=(vmem(), vmem(), vmem()),
        name="order",
    )(action.reshape(1, BELIEFS), index)
    keep, send = pl.pallas_call(
        main_kernel,
        grid=(STEPS,),
        out_shape=(
            jax.ShapeDtypeStruct((ROWS, 512), jnp.float32),
            jax.ShapeDtypeStruct((ROWS, 512), jnp.float32),
        ),
        in_specs=[
            smem(),
            pl.BlockSpec((OBS, CHUNK), lambda i: (0, i), memory_space=pltpu.SMEM),
            smem(),
            vmem(),
            vmem(),
            vmem(),
            vmem(),
            vmem(),
        ],
        out_specs=(vmem(), vmem()),
        scratch_shapes=[
            pltpu.VMEM((ALPHAS * SUB, 128), jnp.float32),
            pltpu.VMEM((ACTS * OBS * SUB, 128), jnp.float32),
            pltpu.VMEM((16 * SUB, 128), jnp.float32),
            pltpu.VMEM((CHUNK, COLS), jnp.bfloat16),
            pltpu.VMEM((ROWS, BELIEFS), jnp.float32),
        ],
        compiler_params=pltpu.CompilerParams(vmem_limit_bytes=50 * 2**20),
        name="mix",
    )(
        core.reshape(1),
        table,
        owner,
        owner,
        target,
        alphas,
        observe.reshape(ACTS * OBS, COLS),
        transitions.reshape(ACTS * ROWS, COLS),
    )
    across = [(0, 1), (1, 0)]
    half = keep + lax.ppermute(send, "co", across)
    mine = lax.dynamic_slice_in_dim(half, high * 256, 256, 1)
    theirs = lax.dynamic_slice_in_dim(half, (1 - high) * 256, 256, 1).astype(jnp.bfloat16)
    summed = mine + lax.ppermute(theirs, "yh", across).astype(jnp.float32)
    row_action = lax.dynamic_slice_in_dim(action, (2 * high + core) * 256, 256)
    picked = (row_action[:, None] == jnp.arange(ACTS, dtype=jnp.int32)[None, :]).astype(jnp.bfloat16)
    gained = jnp.dot(picked, reward, preferred_element_type=jnp.float32)
    return (gained + DISCOUNT / S * summed.T).astype(jnp.bfloat16)


def solution(mesh):
    torus = Mesh(mesh.devices.reshape(8, 4, 2, 2, 2), ("z", "x", "yl", "yh", "co"))
    st = ("yh", "co")
    in_specs = (
        P(None, st),
        P(None, BEL, st),
        P(None, None, st),
        P(None, BEL),
        P(BEL, None, None),
        P(),
    )
    return jax.shard_map(body, mesh=torus, in_specs=in_specs, out_specs=P(st, BEL), check_vma=False)
```

time: 266 us -> 136 us (0.51)
  waiting for transfers between devices: 117 us -> 13.3 us
  Pallas kernels: 0 us -> 93.3 us
  local copies, waits for them, and re-layouts: 67 us -> 6.81 us
  matrix products: 28.9 us -> 0.27 us
  loops' own time: 17.2 us -> 0 us
  starting transfers between devices: 5.16 us -> 19 us
  between operations: 13.5 us -> 0.08 us
  other arithmetic: 11.3 us -> 2.74 us
  blocking collectives: 4.88 us -> 0 us
    all_gather x2 -> x0, waiting for transfers between devices: 105 us -> none  [stacked_from(): blocks = lax.all_gather(blocks, axes[k])]
    pallas_call x0 -> x2, Pallas kernels: none -> 93.3 us  [the longest x1 90.7 us: body(): pl.pallas_call(main_kernel, grid=(STEPS,), out_shape=(jax.ShapeDtypeStruc...]
    gather x4 -> x0, local copies, waits for them, and re-layouts: 45.2 us -> none  [the longest x1 29.4 us: grouped_product(): padded = rows[source].reshape(blocks, block, rows.shape[1])]
    dot_general x10 -> x1, matrix products: 28.9 us -> 0.27 us  [body(): gained = jnp.dot(picked, reward, preferred_element_type=jnp.float32)]
    another operation x1 -> x0, loops' own time: 17.2 us -> none  [grouped_product(): lax.map(one_block, (padded, owner))]
    all_to_all x1, starting transfers between devices: 5.12 us -> 13.5 us  [body(): index = lax.all_to_all(spread, BEL, 0, 0, tiled=True)]
    transpose x1 -> x0, local copies, waits for them, and re-layouts: 6.17 us -> none  [stacked_from(): blocks = blocks.transpose(*back, *range(len(axes), blocks.ndim))]
    dot_general x1 -> x0, other arithmetic: 5.75 us -> none  [mixture_block(): jnp.einsum('bos,bos->bs', picked, weights, preferred_element_type=jnp.flo...]
  transfers between devices with their start and end apart: 3 -> 3, of which waited for: 3 -> 3; matrix products, arithmetic and copies ran while one was open for 3% -> 1% of each run, Pallas kernels for 0% -> 0%
where the time goes in v1:
time: 136 us; the launch traced here: 135 us
  Pallas kernels  93.3 us (69%)
  starting transfers between devices  19 us (14%)
  waiting for transfers between devices  13.3 us (10%)
  local copies, waits for them, and re-layouts  6.81 us (5%)
  other arithmetic  2.74 us (2%)
    pallas_call x1, Pallas kernels, body(): pl.pallas_call(main_kernel, grid=(STEPS,), out_shape=(jax.ShapeDtypeStruc...  90.7 us
    all_to_all x1, starting transfers between devices, body(): index = lax.all_to_all(spread, BEL, 0, 0, tiled=True)  13.5 us
    all_to_all x1, waiting for transfers between devices, body(): index = lax.all_to_all(spread, BEL, 0, 0, tiled=True)  10.2 us
    unnamed x12, local copies, waits for them, and re-layouts  3.74 us
    ppermute x1, starting transfers between devices, body(): half = keep + lax.ppermute(send, 'co', across)  2.78 us
  transfers between devices with their start and end apart: 3, of which 3 were waited for; matrix products, arithmetic and copies ran while one was open for 1% of the time, Pallas kernels for 0%

profile of v1, /device:TPU:1, one launch (start us, length us, event | category | flops | bytes accessed | tf_op | source)
XLA Modules:
  0.0 135.5 jit_solution(257932154445671642)
XLA Ops:
  0.0 0.0 copy-start
  0.0 0.0 copy-start.1
  0.0 0.9 dynamic_slice.13
  0.9 0.9 select_reduce_fusion
  1.8 1.2 reshape.43
  3.0 13.5 %all-to-all-start = ((s32[64,1,768]{2,1,0:T(1,128)}), s32[64,1,768]{2,1,0:T(1,128)S(1)}, u32[]{:S(2)}, u32[]{:S(2)}) async-start(s32[64,1,768]{2,1,0:T(1,128)} %reshape.43), calls=%async_computation | async-start | bytes 393216 | tf_op jit(solution)/shard_map/all_to_all | solution.py:176
  16.5 10.2 %all-to-all-done = s32[64,1,768]{2,1,0:T(1,128)S(1)} async-done(((s32[64,1,768]{2,1,0:T(1,128)}), s32[64,1,768]{2,1,0:T(1,128)S(1)}, u32[]{:S(2)}, u32[]{:S(2)}) %all-to-all-start) | async-done | bytes 196640 | tf_op jit(solution)/shard_map/all_to_all | solution.py:176
  26.7 0.5 broadcast.18
  27.2 1.1 reduce
  28.3 0.3 reshape.44
  28.6 0.9 copy.7
  29.4 2.6 %order.1 = (s32[48,1024]{1,0:T(8,128)}, s32[1,1024]{1,0:T(1,128)}, s32[1,1024]{1,0:T(1,128)}) custom-call(s32[1,1024]{1,0:T(1,128)} %bitcast.15, s32[48,1024]{1,0:T(8,128)} %bitcast.14), custom_call_target="tpu_custom_call" | custom-call | tf_op jit(solution)/shard_map/order/pallas_call | solution.py:178
  32.0 0.0 copy-done.1
  32.0 0.0 copy-start.2
  32.0 0.9 copy-done.2
  33.0 0.0 copy-start.3
  33.0 0.7 copy-done.3
  33.7 0.0 copy-start.4
  33.7 0.7 copy-done.4
  34.3 90.7 %mix.1 = (f32[192,512]{1,0:T(8,128)S(1)}, f32[192,512]{1,0:T(8,128)S(1)}) custom-call(s32[1]{0:T(128)} %bitcast.core_ref, s32[48,1024]{1,0:T(8,128)S(1)} %copy-done.2, s32[1,1024]{1,0:T(1,128)S(1)} %copy-done.3, s32[1,1024]{1,0:T(1,128)S(1)} %copy-done.3, s32[1,1024]{1,0:T(1,128)S(1)} %copy-done.4, bf16[512,3072]{1,0:T(8,128)(2,1)} %alphas_ref.1, ...), custom_call_target="tpu_custom_call" | custom-call | tf_op jit(solution)/shard_map/mix/pallas_call | solution.py:189
  125.0 2.8 %collective-permute-start = (f32[192,512]{1,0:T(8,128)S(1)}, f32[192,512]{1,0:T(8,128)S(1)}, u32[]{:S(2)}, u32[]{:S(2)}) collective-permute-start(f32[192,512]{1,0:T(8,128)S(1)} %get-tuple-element.14), channel_id=1, source_target_pairs={{0,1},{1,0},{2,3},{3,2},{4,5},{5,4},{6,7},{7,6},{8,9},{9,8},{10,11... | collective-permute-start | bytes 1179656 | tf_op jit(solution)/shard_map/ppermute | solution.py:227
  127.8 0.8 dynamic_slice.12
  128.5 0.6 collective-permute-done
  129.1 0.1 add.35
  129.2 2.7 %collective-permute-start.1 = (bf16[192,256]{1,0:T(8,128)(2,1)S(1)}, bf16[192,256]{1,0:T(8,128)(2,1)S(1)}, u32[]{:S(2)}, u32[]{:S(2)}) collective-permute-start(bf16[192,256]{1,0:T(8,128)(2,1)S(1)} %dynamic-slice_convert_fusion), channel_id=1, source_target_pairs={{0,2},{2,0},{1,3},{3,1},{4,6},{6,4},{5,7},{7,5},{8,10},{10,8},{9,1... | collective-permute-start | bytes 294920 | tf_op jit(solution)/shard_map/ppermute | solution.py:230
  131.9 0.0 copy-done
  131.9 0.3 fusion.1
  132.2 2.6 %collective-permute-done.1 = bf16[192,256]{1,0:T(8,128)(2,1)S(1)} collective-permute-done((bf16[192,256]{1,0:T(8,128)(2,1)S(1)}, bf16[192,256]{1,0:T(8,128)(2,1)S(1)}, u32[]{:S(2)}, u32[]{:S(2)}) %collective-permute-start.1) | collective-permute-done | bytes 98336 | tf_op jit(solution)/shard_map/ppermute | solution.py:230
  134.8 0.7 fusion
  (3 shorter events, 0.1 us)
Async XLA Ops:
  0.0 131.9 %copy-start = (bf16[6,192]{1,0:T(8,128)(2,1)S(1)}, bf16[6,192]{1,0:T(8,128)(2,1)}, u32[]{:S(2)}) copy-start(bf16[6,192]{1,0:T(8,128)(2,1)} %param.9) | copy-start | bytes 6916
  0.0 32.0 %copy-start.1 = (bf16[6,48,3072]{2,1,0:T(8,128)(2,1)S(1)}, bf16[6,48,3072]{2,1,0:T(8,128)(2,1)}, u32[]{:S(2)}) copy-start(bf16[6,48,3072]{2,1,0:T(8,128)(2,1)} %param.8) | copy-start | bytes 5308420
  3.0 23.6 %all-to-all-start = ((s32[64,1,768]{2,1,0:T(1,128)}), s32[64,1,768]{2,1,0:T(1,128)S(1)}, u32[]{:S(2)}, u32[]{:S(2)}) async-start(s32[64,1,768]{2,1,0:T(1,128)} %reshape.43), calls=%async_computation | async-start | bytes 393216 | tf_op jit(solution)/shard_map/all_to_all | solution.py:176
  32.0 0.9 copy-start.2
  33.0 0.7 copy-start.3
  33.7 0.7 copy-start.4
  125.0 4.1 %collective-permute-start = (f32[192,512]{1,0:T(8,128)S(1)}, f32[192,512]{1,0:T(8,128)S(1)}, u32[]{:S(2)}, u32[]{:S(2)}) collective-permute-start(f32[192,512]{1,0:T(8,128)S(1)} %get-tuple-element.14), channel_id=1, source_target_pairs={{0,1},{1,0},{2,3},{3,2},{4,5},{5,4},{6,7},{7,6},{8,9},{9,8},{10,11... | collective-permute-start | bytes 1179656 | tf_op jit(solution)/shard_map/ppermute | solution.py:227
  129.2 5.6 %collective-permute-start.1 = (bf16[192,256]{1,0:T(8,128)(2,1)S(1)}, bf16[192,256]{1,0:T(8,128)(2,1)S(1)}, u32[]{:S(2)}, u32[]{:S(2)}) collective-permute-start(bf16[192,256]{1,0:T(8,128)(2,1)S(1)} %dynamic-slice_convert_fusion), channel_id=1, source_target_pairs={{0,2},{2,0},{1,3},{3,1},{4,6},{6,4},{5,7},{7,5},{8,10},{10,8},{9,1... | collective-permute-start | bytes 294920 | tf_op jit(solution)/shard_map/ppermute | solution.py:230

commit v2 on v0

v2 whole, which is shorter than its diff:
```python
import jax
import jax.numpy as jnp
from jax import lax
from jax.experimental import pallas as pl
from jax.experimental.pallas import tpu as pltpu
from jax.sharding import Mesh
from jax.sharding import PartitionSpec as P

S = 12288
ACTS = 6
OBS = 48
ALPHAS = 512
BELIEFS = 1024
BEL = ("z", "x", "yl")
PEERS = 64
OWN = BELIEFS // PEERS
COLS = 3072
ROWS = 192
HALF = COLS // 128
LINES = 2 * HALF
PITCH = 64
GAP = 56
PART = 256
DISCOUNT = 0.95

NT = (((1,), (1,)), ((), ()))


def prep_kernel(alphas_ref, alphas2_ref, observe_ref, observe2_ref, rows_ref, obs_ref, wide_ref):
    def spread(sources, dest):
        def body(k, _):
            at = pl.multiple_of(k * 16, 16)
            for s, source in enumerate(sources):
                for j in range(HALF):
                    part = source[pl.ds(at, 16), j * 128 : (j + 1) * 128]
                    wide_ref[pl.ds(s * HALF + j, 16, stride=GAP), :] = part.astype(jnp.float32)
            for r in range(16):
                dest[at + r, :LINES, :] = wide_ref[r * GAP : r * GAP + LINES, :].astype(jnp.bfloat16)
            return 0

        lax.fori_loop(0, sources[0].shape[0] // 16, body, 0)

    spread((alphas_ref, alphas2_ref), rows_ref)
    spread((observe_ref, observe2_ref), obs_ref)


def main_kernel(
    side_ref, index_ref, action_ref, owner_ref, rows_ref, obs_ref, here_ref, there_ref,
    send_ref, keep_ref, index_smem, weights_ref, mix_ref, block_ref, weight_sems, index_sem,
):
    fetch = [
        pltpu.make_async_copy(source, weights_ref.at[n], weight_sems.at[n])
        for n, source in enumerate((here_ref, there_ref))
    ]
    table = pltpu.make_async_copy(index_ref, index_smem, index_sem)
    table.start()
    for copy in fetch:
        copy.start()
    table.wait()
    high = side_ref[0]
    core = side_ref[1]

    for turn, out_ref in enumerate((send_ref, keep_ref)):
        yh = (1 - high) if turn == 0 else high
        block = 2 * yh + core

        def sixteen(i, _):
            source = block * 16 + i
            for h in range(2):
                for r in range(8):
                    a = action_ref[source * 16 + h * 8 + r]
                    total = None
                    for o in range(OBS):
                        k = index_smem[source, r, h * OBS + o]
                        term = rows_ref[k, :LINES, :].astype(jnp.float32) * obs_ref[a * OBS + o, :LINES, :].astype(jnp.float32)
                        total = term if o == 0 else total + term
                    mix_ref[(h * 8 + r) * GAP : (h * 8 + r) * GAP + LINES, :] = total
            for j in range(LINES):
                part = mix_ref[pl.ds(j, 16, stride=GAP), :]
                block_ref[j // HALF, pl.ds(pl.multiple_of(i * 16, 16), 16), (j % HALF) * 128 : (j % HALF + 1) * 128] = part.astype(jnp.bfloat16)
            return 0

        lax.fori_loop(0, PART // 16, sixteen, 0)
        if turn == 0:
            for copy in fetch:
                copy.wait()
        owner = owner_ref[:, pl.ds(pl.multiple_of(block * PART, 128), PART)]
        value = jnp.zeros((ROWS, PART), jnp.float32)
        for a in range(ACTS):
            got = sum(
                lax.dot_general(
                    weights_ref[n, a * ROWS : (a + 1) * ROWS, :], block_ref[n], NT, preferred_element_type=jnp.float32
                )
                for n in range(2)
            )
            value = jnp.where(owner == a, got, value)
        out_ref[...] = value.astype(out_ref.dtype)


def vmem():
    return pl.BlockSpec(memory_space=pltpu.VMEM)


def smem():
    return pl.BlockSpec(memory_space=pltpu.SMEM)


def anyspace():
    return pl.BlockSpec(memory_space=pl.ANY)


def body(alphas, transitions, observe, reward, belief_index, action):
    bel = lax.axis_index(BEL)
    core = lax.axis_index("co")
    high = lax.axis_index("yh")
    across = [(0, 1), (1, 0)]
    observe = observe.reshape(ACTS * OBS, COLS)
    transitions = transitions.reshape(ACTS * ROWS, COLS)
    alphas2, observe2, transitions2 = (lax.ppermute(v, "co", across) for v in (alphas, observe, transitions))
    own_action = lax.dynamic_slice_in_dim(action, bel * OWN, OWN)
    onehot = own_action[:, None] == jnp.arange(ACTS, dtype=jnp.int32)[None, :]
    chosen = jnp.sum(jnp.where(onehot[:, :, None], belief_index, 0), axis=1)
    packed = jnp.concatenate([chosen[:8], chosen[8:], jnp.zeros((8, 32), jnp.int32)], axis=1)
    index = lax.all_to_all(jnp.tile(packed, (PEERS, 1)), BEL, 0, 0, tiled=True)
    rows, obs = pl.pallas_call(
        prep_kernel,
        out_shape=(
            jax.ShapeDtypeStruct((ALPHAS, PITCH, 128), jnp.bfloat16),
            jax.ShapeDtypeStruct((ACTS * OBS, LINES, 128), jnp.bfloat16),
        ),
        in_specs=[vmem()] * 4,
        out_specs=(vmem(),) * 2,
        scratch_shapes=[pltpu.VMEM((16 * GAP, 128), jnp.float32)],
        compiler_params=pltpu.CompilerParams(vmem_limit_bytes=24 * 2**20),
        cost_estimate=pl.CostEstimate(flops=8 * 10**9, bytes_accessed=10**7, transcendentals=0),
        name="prep",
    )(alphas, alphas2, observe, observe2)
    send, keep = pl.pallas_call(
        main_kernel,
        out_shape=(
            jax.ShapeDtypeStruct((ROWS, PART), jnp.bfloat16),
            jax.ShapeDtypeStruct((ROWS, PART), jnp.float32),
        ),
        in_specs=[smem(), vmem(), smem(), vmem(), vmem(), vmem(), anyspace(), anyspace()],
        out_specs=(vmem(), vmem()),
        scratch_shapes=[
            pltpu.SMEM((PEERS, 8, 128), jnp.int32),
            pltpu.VMEM((2, ACTS * ROWS, COLS), jnp.bfloat16),
            pltpu.VMEM((16 * GAP, 128), jnp.float32),
            pltpu.VMEM((2, PART, COLS), jnp.bfloat16),
            pltpu.SemaphoreType.DMA((2,)),
            pltpu.SemaphoreType.DMA,
        ],
        compiler_params=pltpu.CompilerParams(vmem_limit_bytes=40 * 2**20),
        name="mix",
    )(
        jnp.stack([high, core]),
        index.reshape(PEERS, 8, 128),
        action,
        action.reshape(1, BELIEFS),
        rows,
        obs,
        transitions,
        transitions2,
    )
    summed = keep + lax.ppermute(send, "yh", across).astype(jnp.float32)
    row_action = lax.dynamic_slice_in_dim(action, (2 * high + core) * PART, PART)
    picked = (row_action[:, None] == jnp.arange(ACTS, dtype=jnp.int32)[None, :]).astype(jnp.bfloat16)
    gained = jnp.dot(picked, reward, preferred_element_type=jnp.float32)
    return (gained + DISCOUNT / S * summed.T).astype(jnp.bfloat16)


def solution(mesh):
    torus = Mesh(mesh.devices.reshape(8, 4, 2, 2, 2), ("z", "x", "yl", "yh", "co"))
    st = ("yh", "co")
    in_specs = (
        P(None, st),
        P(None, BEL, st),
        P(None, None, st),
        P(None, BEL),
        P(BEL, None, None),
        P(),
    )
    return jax.shard_map(body, mesh=torus, in_specs=in_specs, out_specs=P(st, BEL), check_vma=False)
```

time: 266 us -> 109 us (0.41)
  waiting for transfers between devices: 117 us -> 7.13 us
  Pallas kernels: 0 us -> 67.2 us
  local copies, waits for them, and re-layouts: 67 us -> 15.5 us
  matrix products: 28.9 us -> 0.27 us
  loops' own time: 17.2 us -> 0 us
  between operations: 13.5 us -> 0.09 us
  starting transfers between devices: 5.16 us -> 16.2 us
  other arithmetic: 11.3 us -> 1.71 us
  blocking collectives: 4.88 us -> 0 us
    all_gather x2 -> x0, waiting for transfers between devices: 105 us -> none  [stacked_from(): blocks = lax.all_gather(blocks, axes[k])]
    pallas_call x0 -> x2, Pallas kernels: none -> 67.2 us  [the longest x1 61.9 us: body(): pl.pallas_call(main_kernel, out_shape=(jax.ShapeDtypeStruct((ROWS, PART),...]
    gather x4 -> x0, local copies, waits for them, and re-layouts: 45.2 us -> none  [the longest x1 29.4 us: grouped_product(): padded = rows[source].reshape(blocks, block, rows.shape[1])]
    dot_general x10 -> x1, matrix products: 28.9 us -> 0.27 us  [body(): gained = jnp.dot(picked, reward, preferred_element_type=jnp.float32)]
    another operation x1 -> x0, loops' own time: 17.2 us -> none  [grouped_product(): lax.map(one_block, (padded, owner))]
    unnamed x6 -> x16, local copies, waits for them, and re-layouts: 0.01 us -> 13.1 us
    all_to_all x1, waiting for transfers between devices: 12.2 us -> 0.01 us  [body(): index = lax.all_to_all(jnp.tile(packed, (PEERS, 1)), BEL, 0, 0, tiled=True)]
    ppermute x0 -> x4, waiting for transfers between devices: none -> 7.13 us  [the longest x1 3.99 us: body(): summed = keep + lax.ppermute(send, 'yh', across).astype(jnp.float32)]
  transfers between devices with their start and end apart: 3 -> 5, of which waited for: 3 -> 2; matrix products, arithmetic and copies ran while one was open for 3% -> 3% of each run, Pallas kernels for 0% -> 5%
where the time goes in v2:
time: 109 us; the launch traced here: 108 us
  Pallas kernels  67.2 us (62%)
  starting transfers between devices  16.2 us (15%)
  local copies, waits for them, and re-layouts  15.5 us (14%)
  waiting for transfers between devices  7.13 us (7%)
  other arithmetic  1.71 us (2%)
    pallas_call x1, Pallas kernels, body(): pl.pallas_call(main_kernel, out_shape=(jax.ShapeDtypeStruct((ROWS, PART),...  61.9 us
    unnamed x16, local copies, waits for them, and re-layouts  13.1 us
    all_to_all x1, starting transfers between devices, body(): index = lax.all_to_all(jnp.tile(packed, (PEERS, 1)), BEL, 0, 0, tiled=True)  11.2 us
    pallas_call x1, Pallas kernels, body(): pl.pallas_call(prep_kernel, out_shape=(jax.ShapeDtypeStruct((ALPHAS, PITC...  5.31 us
    ppermute x1, waiting for transfers between devices, body(): summed = keep + lax.ppermute(send, 'yh', across).astype(jnp.float32)  3.99 us
    ppermute x3, starting transfers between devices, body(): lax.ppermute(v, 'co', across)  3.71 us
    ppermute x3, waiting for transfers between devices, body(): lax.ppermute(v, 'co', across)  3.14 us
  transfers between devices with their start and end apart: 5, of which 2 were waited for; matrix products, arithmetic and copies ran while one was open for 3% of the time, Pallas kernels for 5%

profile of v2, /device:TPU:1, one launch (start us, length us, event | category | flops | bytes accessed | tf_op | source)
XLA Modules:
  0.0 108.1 jit_solution(4932342617203301629)
XLA Ops:
  0.0 0.0 copy-start
  0.0 3.2 %collective-permute-start.2 = (bf16[1152,3072]{1,0:T(8,128)(2,1)}, bf16[1152,3072]{1,0:T(8,128)(2,1)}, u32[]{:S(2)}, u32[]{:S(2)}) collective-permute-start(bf16[1152,3072]{1,0:T(8,128)(2,1)} %bitcast.10), channel_id=1, source_target_pairs={{0,1},{1,0},{2,3},{3,2},{4,5},{5,4},{6,7},{7,6},{8,9},{9,8},{10,11... | collective-permute-start | bytes 21233672 | tf_op jit(solution)/shard_map/ppermute | solution.py:119
  3.2 0.0 collective-permute-start
  3.2 0.5 collective-permute-start.1
  3.7 0.1 pad.2.clone
  3.8 0.8 dynamic_slice.7
  4.6 0.9 select_reduce_fusion
  5.5 0.1 add_add_fusion
  5.5 0.7 tile.2
  6.3 11.2 %all-to-all-start = ((s32[64,8,128]{2,1,0:T(8,128)}), s32[64,8,128]{2,1,0:T(8,128)}, u32[]{:S(2)}, u32[]{:S(2)}) async-start(s32[64,8,128]{2,1,0:T(8,128)} %tile.2), calls=%async_computation | async-start | bytes 524288 | tf_op jit(solution)/shard_map/all_to_all | solution.py:124
  17.5 0.8 dynamic_slice.6
  18.3 0.1 pad_add_fusion.side_ref
  18.4 3.1 %collective-permute-done.1.observe2_ref = bf16[288,3072]{1,0:T(8,128)(2,1)} collective-permute-done((bf16[288,3072]{1,0:T(8,128)(2,1)}, bf16[288,3072]{1,0:T(8,128)(2,1)}, u32[]{:S(2)}, u32[]{:S(2)}) %collective-permute-start.1) | collective-permute-done | bytes 1769504 | tf_op jit(solution)/shard_map/ppermute | solution.py:119
  21.5 0.0 collective-permute-done.alphas2_ref
  21.5 1.6 %copy-done.5 = bf16[512,3072]{1,0:T(8,128)(2,1)} copy-done((bf16[512,3072]{1,0:T(8,128)(2,1)}, bf16[512,3072]{1,0:T(8,128)(2,1)S(1)}, u32[]{:S(2)}) %copy-start.5) | copy-done | bytes 3145752
  23.1 1.9 %copy-done.4 = bf16[512,3072]{1,0:T(8,128)(2,1)S(1)} copy-done((bf16[512,3072]{1,0:T(8,128)(2,1)S(1)}, bf16[512,3072]{1,0:T(8,128)(2,1)}, u32[]{:S(2)}) %copy-start.4) | copy-done | bytes 3145752
  25.0 1.9 %copy-done.6 = bf16[512,3072]{1,0:T(8,128)(2,1)S(1)} copy-done((bf16[512,3072]{1,0:T(8,128)(2,1)S(1)}, bf16[512,3072]{1,0:T(8,128)(2,1)}, u32[]{:S(2)}) %copy-start.6) | copy-done | bytes 3145752
  26.9 1.5 %copy-done.7 = bf16[6,48,3072]{2,1,0:T(8,128)(2,1)S(1)} copy-done((bf16[6,48,3072]{2,1,0:T(8,128)(2,1)S(1)}, bf16[6,48,3072]{2,1,0:T(8,128)(2,1)}, u32[]{:S(2)}) %copy-start.7) | copy-done | bytes 1769496
  28.4 5.3 %prep.1 = (bf16[512,64,128]{2,1,0:T(8,128)(2,1)S(1)}, bf16[288,48,128]{2,1,0:T(8,128)(2,1)S(1)}) custom-call(bf16[512,3072]{1,0:T(8,128)(2,1)S(1)} %copy-done.4, bf16[512,3072]{1,0:T(8,128)(2,1)S(1)} %copy-done.6, bf16[288,3072]{1,0:T(8,128)(2,1)S(1)} %bitcast.14, bf16[288,3072]{1,0:T(8,128)(2,1)} %collective-permute-done.1.observe2_ref), custom_call_target="tpu_custom_call" | custom-call | flops 8000000000 | bytes 10000000 | tf_op jit(solution)/shard_map/prep/pallas_call | solution.py:125
  33.7 0.0 copy-start.1
  33.7 3.2 %copy-done.1 = bf16[512,64,128]{2,1,0:T(8,128)(2,1)} copy-done((bf16[512,64,128]{2,1,0:T(8,128)(2,1)}, bf16[512,64,128]{2,1,0:T(8,128)(2,1)S(1)}, u32[]{:S(2)}) %copy-start.1) | copy-done | bytes 8388632
  36.9 0.0 all-to-all-done.index_ref
  36.9 0.0 collective-permute-done.2.there_ref
  36.9 0.0 copy-done.3
  36.9 0.0 copy-start.2
  36.9 3.0 %copy-done.2 = bf16[6,192,3072]{2,1,0:T(8,128)(2,1)S(1)} copy-done((bf16[6,192,3072]{2,1,0:T(8,128)(2,1)S(1)}, bf16[6,192,3072]{2,1,0:T(8,128)(2,1)}, u32[]{:S(2)}) %copy-start.2) | copy-done | bytes 7077912
  39.9 61.9 %mix.1 = (bf16[192,256]{1,0:T(8,128)(2,1)S(1)}, f32[192,256]{1,0:T(8,128)S(1)}) custom-call(s32[2]{0:T(128)S(1)} %pad_add_fusion.side_ref, s32[64,8,128]{2,1,0:T(8,128)} %all-to-all-done.index_ref, s32[1024]{0:T(1024)S(1)} %copy-done.3, s32[1,1024]{1,0:T(1,128)S(1)} %bitcast.12, bf16[512,64,128]{2,1,0:T(8,128)(2,1)} %copy-done.1, ...), custom_call_target="tpu_custom_call" | custom-call | tf_op jit(solution)/shard_map/mix/pallas_call | solution.py:138
  101.8 1.3 %collective-permute-start.3 = (bf16[192,256]{1,0:T(8,128)(2,1)S(1)}, bf16[192,256]{1,0:T(8,128)(2,1)S(1)}, u32[]{:S(2)}, u32[]{:S(2)}) collective-permute-start(bf16[192,256]{1,0:T(8,128)(2,1)S(1)} %get-tuple-element.12), channel_id=1, source_target_pairs={{0,2},{2,0},{1,3},{3,1},{4,6},{6,4},{5,7},{7,5},{8,10},{10,8},{9,1... | collective-permute-start | bytes 294920 | tf_op jit(solution)/shard_map/ppermute | solution.py:166
  103.1 0.0 copy-done
  103.1 0.3 fusion.1
  103.4 4.0 %collective-permute-done.3 = bf16[192,256]{1,0:T(8,128)(2,1)S(1)} collective-permute-done((bf16[192,256]{1,0:T(8,128)(2,1)S(1)}, bf16[192,256]{1,0:T(8,128)(2,1)S(1)}, u32[]{:S(2)}, u32[]{:S(2)}) %collective-permute-start.3) | collective-permute-done | bytes 98336 | tf_op jit(solution)/shard_map/ppermute | solution.py:166
  107.4 0.7 fusion
  (8 shorter events, 0.0 us)
Async XLA Ops:
  0.0 103.1 %copy-start = (bf16[6,192]{1,0:T(8,128)(2,1)S(1)}, bf16[6,192]{1,0:T(8,128)(2,1)}, u32[]{:S(2)}) copy-start(bf16[6,192]{1,0:T(8,128)(2,1)} %param.9) | copy-start | bytes 6916
  0.0 36.9 %collective-permute-start.2 = (bf16[1152,3072]{1,0:T(8,128)(2,1)}, bf16[1152,3072]{1,0:T(8,128)(2,1)}, u32[]{:S(2)}, u32[]{:S(2)}) collective-permute-start(bf16[1152,3072]{1,0:T(8,128)(2,1)} %bitcast.10), channel_id=1, source_target_pairs={{0,1},{1,0},{2,3},{3,2},{4,5},{5,4},{6,7},{7,6},{8,9},{9,8},{10,11... | collective-permute-start | bytes 21233672 | tf_op jit(solution)/shard_map/ppermute | solution.py:119
  3.2 18.3 %collective-permute-start = (bf16[512,3072]{1,0:T(8,128)(2,1)}, bf16[512,3072]{1,0:T(8,128)(2,1)S(1)}, u32[]{:S(2)}, u32[]{:S(2)}) collective-permute-start(bf16[512,3072]{1,0:T(8,128)(2,1)} %alphas_ref.1), channel_id=1, source_target_pairs={{0,1},{1,0},{2,3},{3,2},{4,5},{5,4},{6,7},{7,6},{8,9},{9,8},{10,11... | collective-permute-start | bytes 9437192 | tf_op jit(solution)/shard_map/ppermute | solution.py:119
  3.2 18.3 %collective-permute-start.1 = (bf16[288,3072]{1,0:T(8,128)(2,1)}, bf16[288,3072]{1,0:T(8,128)(2,1)}, u32[]{:S(2)}, u32[]{:S(2)}) collective-permute-start(bf16[288,3072]{1,0:T(8,128)(2,1)} %bitcast.13), channel_id=1, source_target_pairs={{0,1},{1,0},{2,3},{3,2},{4,5},{5,4},{6,7},{7,6},{8,9},{9,8},{10,11... | collective-permute-start | bytes 5308424 | tf_op jit(solution)/shard_map/ppermute | solution.py:119
  6.3 30.7 %all-to-all-start = ((s32[64,8,128]{2,1,0:T(8,128)}), s32[64,8,128]{2,1,0:T(8,128)}, u32[]{:S(2)}, u32[]{:S(2)}) async-start(s32[64,8,128]{2,1,0:T(8,128)} %tile.2), calls=%async_computation | async-start | bytes 524288 | tf_op jit(solution)/shard_map/all_to_all | solution.py:124
  18.4 18.6 %copy-start.3 = (s32[1024]{0:T(1024)S(1)}, s32[1024]{0:T(1024)}, u32[]{:S(2)}) copy-start(s32[1024]{0:T(1024)} %action_ref.1) | copy-start | bytes 12292
  21.5 1.6 %copy-start.5 = (bf16[512,3072]{1,0:T(8,128)(2,1)}, bf16[512,3072]{1,0:T(8,128)(2,1)S(1)}, u32[]{:S(2)}) copy-start(bf16[512,3072]{1,0:T(8,128)(2,1)S(1)} %collective-permute-done.alphas2_ref) | copy-start | bytes 9437188
  23.1 1.9 %copy-start.4 = (bf16[512,3072]{1,0:T(8,128)(2,1)S(1)}, bf16[512,3072]{1,0:T(8,128)(2,1)}, u32[]{:S(2)}) copy-start(bf16[512,3072]{1,0:T(8,128)(2,1)} %alphas_ref.1) | copy-start | bytes 9437188
  25.0 1.9 %copy-start.6 = (bf16[512,3072]{1,0:T(8,128)(2,1)S(1)}, bf16[512,3072]{1,0:T(8,128)(2,1)}, u32[]{:S(2)}) copy-start(bf16[512,3072]{1,0:T(8,128)(2,1)} %copy-done.5) | copy-start | bytes 9437188
  26.9 1.5 %copy-start.7 = (bf16[6,48,3072]{2,1,0:T(8,128)(2,1)S(1)}, bf16[6,48,3072]{2,1,0:T(8,128)(2,1)}, u32[]{:S(2)}) copy-start(bf16[6,48,3072]{2,1,0:T(8,128)(2,1)} %param.8) | copy-start | bytes 5308420
  33.7 3.2 %copy-start.1 = (bf16[512,64,128]{2,1,0:T(8,128)(2,1)}, bf16[512,64,128]{2,1,0:T(8,128)(2,1)S(1)}, u32[]{:S(2)}) copy-start(bf16[512,64,128]{2,1,0:T(8,128)(2,1)S(1)} %get-tuple-element.9.rows_ref) | copy-start | bytes 25165828
  36.9 3.0 %copy-start.2 = (bf16[6,192,3072]{2,1,0:T(8,128)(2,1)S(1)}, bf16[6,192,3072]{2,1,0:T(8,128)(2,1)}, u32[]{:S(2)}) copy-start(bf16[6,192,3072]{2,1,0:T(8,128)(2,1)} %param.7) | copy-start | bytes 21233668
  101.8 5.6 %collective-permute-start.3 = (bf16[192,256]{1,0:T(8,128)(2,1)S(1)}, bf16[192,256]{1,0:T(8,128)(2,1)S(1)}, u32[]{:S(2)}, u32[]{:S(2)}) collective-permute-start(bf16[192,256]{1,0:T(8,128)(2,1)S(1)} %get-tuple-element.12), channel_id=1, source_target_pairs={{0,2},{2,0},{1,3},{3,1},{4,6},{6,4},{5,7},{7,5},{8,10},{10,8},{9,1... | collective-permute-start | bytes 294920 | tf_op jit(solution)/shard_map/ppermute | solution.py:166

commit v3 on v2

v3 whole, which is shorter than its diff:
```python
import jax
import jax.numpy as jnp
from jax import lax
from jax.experimental import pallas as pl
from jax.experimental.pallas import tpu as pltpu
from jax.sharding import Mesh
from jax.sharding import PartitionSpec as P

S = 12288
ACTS = 6
OBS = 48
ALPHAS = 512
BELIEFS = 1024
BEL = ("z", "x", "yl")
PEERS = 64
OWN = BELIEFS // PEERS
COLS = 3072
ROWS = 192
HALF = COLS // 128
LINES = 2 * HALF
PITCH = 64
GAP = 56
PART = 256
WEIGHTS = ALPHAS * PITCH
TOTAL = WEIGHTS + ACTS * OBS * LINES
STAGE = 32
DISCOUNT = 0.95

NT = (((1,), (1,)), ((), ()))


def prep_kernel(alphas_ref, alphas2_ref, observe_ref, observe2_ref, lines_ref, stage_ref, wide_ref, sems):
    counts = [ALPHAS // STAGE, ACTS * OBS // STAGE]

    def spread(sources, steps, first, pitch):
        def copies(t, slot):
            return [
                pltpu.make_async_copy(
                    source.at[pl.ds(pl.multiple_of(t * STAGE, STAGE), STAGE), :], stage_ref.at[slot, s], sems.at[slot, s]
                )
                for s, source in enumerate(sources)
            ]

        for slot in range(3):
            for copy in copies(slot, slot):
                copy.start()

        def step(t, _):
            slot = lax.rem(t, 4)

            @pl.when(t + 3 < steps)
            def _():
                for copy in copies(t + 3, lax.rem(t + 3, 4)):
                    copy.start()

            for copy in copies(t, slot):
                copy.wait()
            for g in range(STAGE // 16):
                for s in range(2):
                    for j in range(HALF):
                        part = stage_ref[slot, s, g * 16 : (g + 1) * 16, j * 128 : (j + 1) * 128]
                        wide_ref[pl.ds(s * HALF + j, 16, stride=GAP), :] = part.astype(jnp.float32)
                for r in range(16):
                    at = pl.multiple_of(first + (t * STAGE + g * 16 + r) * pitch, 16)
                    lines_ref[pl.ds(at, LINES), :] = wide_ref[r * GAP : r * GAP + LINES, :].astype(jnp.bfloat16)
            return 0

        lax.fori_loop(0, steps, step, 0)

    spread((alphas_ref, alphas2_ref), counts[0], 0, PITCH)
    spread((observe_ref, observe2_ref), counts[1], WEIGHTS, LINES)


def main_kernel(
    side_ref, index_ref, action_ref, owner_ref, source_ref, here_ref, there_ref,
    send_ref, keep_ref, lines_ref, index_smem, weights_ref, mix_ref, block_ref, weight_sems, index_sem, lines_sem,
):
    fetch = [
        pltpu.make_async_copy(source, weights_ref.at[n], weight_sems.at[n])
        for n, source in enumerate((here_ref, there_ref))
    ]
    table = pltpu.make_async_copy(index_ref, index_smem, index_sem)
    lines = pltpu.make_async_copy(source_ref, lines_ref, lines_sem)
    lines.start()
    table.start()
    for copy in fetch:
        copy.start()
    table.wait()
    lines.wait()
    rows_ref = lines_ref.at[pl.ds(0, WEIGHTS), :].reshape(ALPHAS, PITCH, 128)
    obs_ref = lines_ref.at[pl.ds(WEIGHTS, ACTS * OBS * LINES), :].reshape(ACTS * OBS, LINES, 128)
    high = side_ref[0]
    core = side_ref[1]

    def turn(t, _):
        block = 2 * jnp.where(t == 0, 1 - high, high) + core

        def sixteen(i, _):
            source = block * 16 + i
            for h in range(2):
                for r in range(8):
                    a = action_ref[source * 16 + h * 8 + r]
                    total = None
                    for o in range(OBS):
                        k = index_smem[source, r, h * OBS + o]
                        term = rows_ref[k, :LINES, :].astype(jnp.float32) * obs_ref[a * OBS + o].astype(jnp.float32)
                        total = term if o == 0 else total + term
                    mix_ref[(h * 8 + r) * GAP : (h * 8 + r) * GAP + LINES, :] = total
            for j in range(LINES):
                part = mix_ref[pl.ds(j, 16, stride=GAP), :]
                block_ref[j // HALF, pl.ds(pl.multiple_of(i * 16, 16), 16), (j % HALF) * 128 : (j % HALF + 1) * 128] = part.astype(jnp.bfloat16)
            return 0

        lax.fori_loop(0, PART // 16, sixteen, 0)

        @pl.when(t == 0)
        def _():
            for copy in fetch:
                copy.wait()

        got = lax.dot_general(weights_ref[0], block_ref[0], NT, preferred_element_type=jnp.float32)
        got += lax.dot_general(weights_ref[1], block_ref[1], NT, preferred_element_type=jnp.float32)
        owner = owner_ref[:, pl.ds(pl.multiple_of(block * PART, 128), PART)]
        value = got[:ROWS]
        for a in range(1, ACTS):
            value = jnp.where(owner == a, got[a * ROWS : (a + 1) * ROWS], value)

        @pl.when(t == 0)
        def _():
            send_ref[...] = value.astype(send_ref.dtype)

        @pl.when(t == 1)
        def _():
            keep_ref[...] = value

        return 0

    lax.fori_loop(0, 2, turn, 0)


def vmem():
    return pl.BlockSpec(memory_space=pltpu.VMEM)


def smem():
    return pl.BlockSpec(memory_space=pltpu.SMEM)


def hbm():
    return pl.BlockSpec(memory_space=pltpu.HBM)


def body(alphas, transitions, observe, reward, belief_index, action):
    bel = lax.axis_index(BEL)
    core = lax.axis_index("co")
    high = lax.axis_index("yh")
    across = [(0, 1), (1, 0)]
    observe = observe.reshape(ACTS * OBS, COLS)
    transitions = transitions.reshape(ACTS * ROWS, COLS)
    alphas2, observe2 = (lax.ppermute(v, "co", across) for v in (alphas, observe))
    own_action = lax.dynamic_slice_in_dim(action, bel * OWN, OWN)
    onehot = own_action[:, None] == jnp.arange(ACTS, dtype=jnp.int32)[None, :]
    chosen = jnp.sum(jnp.where(onehot[:, :, None], belief_index, 0), axis=1)
    packed = jnp.concatenate([chosen[:8], chosen[8:], jnp.zeros((8, 32), jnp.int32)], axis=1)
    late, packed = lax.optimization_barrier((transitions, packed))
    transitions2 = lax.ppermute(late, "co", across)
    index = lax.all_to_all(jnp.tile(packed, (PEERS, 1)), BEL, 0, 0, tiled=True)
    lines = pl.pallas_call(
        prep_kernel,
        out_shape=jax.ShapeDtypeStruct((TOTAL, 128), jnp.bfloat16),
        in_specs=[hbm()] * 4,
        out_specs=vmem(),
        scratch_shapes=[
            pltpu.VMEM((4, 2, STAGE, COLS), jnp.bfloat16),
            pltpu.VMEM((16 * GAP, 128), jnp.float32),
            pltpu.SemaphoreType.DMA((4, 2)),
        ],
        compiler_params=pltpu.CompilerParams(vmem_limit_bytes=62 * 2**20),
        cost_estimate=pl.CostEstimate(flops=8 * 10**9, bytes_accessed=10**7, transcendentals=0),
        name="prep",
    )(alphas, alphas2, observe, observe2)
    send, keep = pl.pallas_call(
        main_kernel,
        out_shape=(
            jax.ShapeDtypeStruct((ROWS, PART), jnp.bfloat16),
            jax.ShapeDtypeStruct((ROWS, PART), jnp.float32),
        ),
        in_specs=[smem(), vmem(), smem(), vmem(), hbm(), hbm(), hbm()],
        out_specs=(vmem(), vmem()),
        scratch_shapes=[
            pltpu.VMEM((TOTAL, 128), jnp.bfloat16),
            pltpu.SMEM((PEERS, 8, 128), jnp.int32),
            pltpu.VMEM((2, ACTS * ROWS, COLS), jnp.bfloat16),
            pltpu.VMEM((16 * GAP, 128), jnp.float32),
            pltpu.VMEM((2, PART, COLS), jnp.bfloat16),
            pltpu.SemaphoreType.DMA((2,)),
            pltpu.SemaphoreType.DMA,
            pltpu.SemaphoreType.DMA,
        ],
        compiler_params=pltpu.CompilerParams(vmem_limit_bytes=62 * 2**20),
        name="mix",
    )(
        jnp.stack([high, core]),
        index.reshape(PEERS, 8, 128),
        action,
        action.reshape(1, BELIEFS),
        lines,
        transitions,
        transitions2,
    )
    summed = keep + lax.ppermute(send, "yh", across).astype(jnp.float32)
    row_action = lax.dynamic_slice_in_dim(action, (2 * high + core) * PART, PART)
    picked = (row_action[:, None] == jnp.arange(ACTS, dtype=jnp.int32)[None, :]).astype(jnp.bfloat16)
    gained = jnp.dot(picked, reward, preferred_element_type=jnp.float32)
    return (gained + DISCOUNT / S * summed.T).astype(jnp.bfloat16)


def solution(mesh):
    torus = Mesh(mesh.devices.reshape(8, 4, 2, 2, 2), ("z", "x", "yl", "yh", "co"))
    st = ("yh", "co")
    in_specs = (
        P(None, st),
        P(None, BEL, st),
        P(None, None, st),
        P(None, BEL),
        P(BEL, None, None),
        P(),
    )
    return jax.shard_map(body, mesh=torus, in_specs=in_specs, out_specs=P(st, BEL), check_vma=False)
```

time: 109 us -> 96.1 us (0.88)
  local copies, waits for them, and re-layouts: 15.5 us -> 3.04 us
  Pallas kernels: 67.2 us -> 64.2 us
  waiting for transfers between devices: 7.13 us -> 8.84 us
  other arithmetic: 1.71 us -> 3.23 us
    unnamed x16 -> x4, local copies, waits for them, and re-layouts: 13.1 us -> 0.69 us
    pallas_call x1, Pallas kernels: 61.9 us -> 50.7 us  [body(): pl.pallas_call(main_kernel, out_shape=(jax.ShapeDtypeStruct((ROWS, PART),...]
    pallas_call x1, Pallas kernels: 5.31 us -> 13.5 us  [body(): pl.pallas_call(prep_kernel, out_shape=jax.ShapeDtypeStruct((TOTAL, 128),...]
    ppermute x0 -> x1, starting transfers between devices: none -> 3.23 us  [body(): transitions2 = lax.ppermute(late, 'co', across)]
    ppermute x3 -> x2, starting transfers between devices: 3.71 us -> 0.51 us  [body(): lax.ppermute(v, 'co', across)]
    ppermute x3 -> x2, waiting for transfers between devices: 3.14 us -> 4.63 us  [body(): lax.ppermute(v, 'co', across)]
  transfers between devices with their start and end apart: 5 -> 5, of which waited for: 2 -> 2; matrix products, arithmetic and copies ran while one was open for 3% -> 3% of each run, Pallas kernels for 5% -> 14%
where the time goes in v3:
time: 96.1 us; the launch traced here: 95.7 us
  Pallas kernels  64.2 us (67%)
  starting transfers between devices  16 us (17%)
  waiting for transfers between devices  8.84 us (9%)
  other arithmetic  3.23 us (3%)
  local copies, waits for them, and re-layouts  3.04 us (3%)
    pallas_call x1, Pallas kernels, body(): pl.pallas_call(main_kernel, out_shape=(jax.ShapeDtypeStruct((ROWS, PART),...  50.7 us
    pallas_call x1, Pallas kernels, body(): pl.pallas_call(prep_kernel, out_shape=jax.ShapeDtypeStruct((TOTAL, 128),...  13.5 us
    all_to_all x1, starting transfers between devices, body(): index = lax.all_to_all(jnp.tile(packed, (PEERS, 1)), BEL, 0, 0, tiled=True)  11 us
    ppermute x2, waiting for transfers between devices, body(): lax.ppermute(v, 'co', across)  4.63 us
    ppermute x1, waiting for transfers between devices, body(): summed = keep + lax.ppermute(send, 'yh', across).astype(jnp.float32)  4.2 us
    ppermute x1, starting transfers between devices, body(): transitions2 = lax.ppermute(late, 'co', across)  3.23 us
  transfers between devices with their start and end apart: 5, of which 2 were waited for; matrix products, arithmetic and copies ran while one was open for 3% of the time, Pallas kernels for 14%

profile of v3, /device:TPU:1, one launch (start us, length us, event | category | flops | bytes accessed | tf_op | source)
XLA Modules:
  0.0 95.7 jit_solution(5931371294855376675)
XLA Ops:
  0.0 0.0 copy-start
  0.0 0.8 dynamic_slice.7
  0.8 0.1 pad.2.clone
  0.9 0.9 select_reduce_fusion
  1.8 0.1 add_add_fusion
  1.8 3.2 %collective-permute-start.2 = (bf16[1152,3072]{1,0:T(8,128)(2,1)}, bf16[1152,3072]{1,0:T(8,128)(2,1)}, u32[]{:S(2)}, u32[]{:S(2)}) collective-permute-start(bf16[1152,3072]{1,0:T(8,128)(2,1)} %bitcast.10), channel_id=1, source_target_pairs={{0,1},{1,0},{2,3},{3,2},{4,5},{5,4},{6,7},{7,6},{8,9},{9,8},{10,11... | collective-permute-start | bytes 21233672 | tf_op jit(solution)/shard_map/ppermute | solution.py:166
  5.1 0.1 collective-permute-start
  5.2 0.4 collective-permute-start.1
  5.6 0.7 tile.2
  6.3 11.0 %all-to-all-start = ((s32[64,8,128]{2,1,0:T(8,128)}), s32[64,8,128]{2,1,0:T(8,128)S(1)}, u32[]{:S(2)}, u32[]{:S(2)}) async-start(s32[64,8,128]{2,1,0:T(8,128)} %tile.2), calls=%async_computation | async-start | bytes 524288 | tf_op jit(solution)/shard_map/all_to_all | solution.py:167
  17.3 0.8 dynamic_slice.6
  18.0 0.7 pad_add_fusion.side_ref
  18.7 4.6 %collective-permute-done.1.observe2_ref = bf16[288,3072]{1,0:T(8,128)(2,1)} collective-permute-done((bf16[288,3072]{1,0:T(8,128)(2,1)}, bf16[288,3072]{1,0:T(8,128)(2,1)}, u32[]{:S(2)}, u32[]{:S(2)}) %collective-permute-start.1) | collective-permute-done | bytes 1769504 | tf_op jit(solution)/shard_map/ppermute | solution.py:160
  23.3 0.0 collective-permute-done.alphas2_ref
  23.4 13.5 %prep.1.source_ref = bf16[46592,128]{1,0:T(8,128)(2,1)} custom-call(bf16[512,3072]{1,0:T(8,128)(2,1)} %alphas_ref.1, bf16[512,3072]{1,0:T(8,128)(2,1)} %collective-permute-done.alphas2_ref, bf16[288,3072]{1,0:T(8,128)(2,1)} %bitcast.14, bf16[288,3072]{1,0:T(8,128)(2,1)} %collective-permute-done.1.observe2_ref), custom_call_target="tpu_custom_call" | custom-call | flops 8000000000 | bytes 10000000 | tf_op jit(solution)/shard_map/prep/pallas_call | solution.py:168
  36.8 0.0 all-to-all-done.index_ref
  36.9 0.0 copy-start.1
  36.9 0.0 collective-permute-done.2.there_ref
  36.9 0.7 copy-done.1
  37.6 50.7 %mix.1 = (bf16[192,256]{1,0:T(8,128)(2,1)}, f32[192,256]{1,0:T(8,128)}) custom-call(s32[2]{0:T(128)} %pad_add_fusion.side_ref, s32[64,8,128]{2,1,0:T(8,128)} %copy-done.1, s32[1024]{0:T(1024)} %action_ref.1, s32[1,1024]{1,0:T(1,128)} %bitcast.12, bf16[46592,128]{1,0:T(8,128)(2,1)} %prep.1.source_ref, bf16[1152,3072]{1,0:T(8,128)(2,1)} %bitcast.11, ...), custom_call_target="tpu_custom_call" | custom-call | tf_op jit(solution)/shard_map/mix/pallas_call | solution.py:182
  88.3 1.3 %collective-permute-start.3 = (bf16[192,256]{1,0:T(8,128)(2,1)}, bf16[192,256]{1,0:T(8,128)(2,1)S(1)}, u32[]{:S(2)}, u32[]{:S(2)}) collective-permute-start(bf16[192,256]{1,0:T(8,128)(2,1)} %get-tuple-element.12), channel_id=1, source_target_pairs={{0,2},{2,0},{1,3},{3,1},{4,6},{6,4},{5,7},{7,5},{8,10},{10,8},{9,1... | collective-permute-start | bytes 294920 | tf_op jit(solution)/shard_map/ppermute | solution.py:211
  89.6 0.0 copy-done
  89.6 0.3 fusion.1
  89.9 4.2 %collective-permute-done.3 = bf16[192,256]{1,0:T(8,128)(2,1)S(1)} collective-permute-done((bf16[192,256]{1,0:T(8,128)(2,1)}, bf16[192,256]{1,0:T(8,128)(2,1)S(1)}, u32[]{:S(2)}, u32[]{:S(2)}) %collective-permute-start.3) | collective-permute-done | bytes 98336 | tf_op jit(solution)/shard_map/ppermute | solution.py:211
  94.1 1.6 %fusion = bf16[256,192]{0,1:T(8,128)(2,1)} fusion(f32[256,192]{0,1:T(8,128)S(1)} %fusion.1, f32[192,256]{1,0:T(8,128)} %get-tuple-element.11, bf16[192,256]{1,0:T(8,128)(2,1)S(1)} %collective-permute-done.3), kind=kLoop, calls=%fused_computation.1 | loop fusion | flops 245760 | bytes 589824 | tf_op jit(solution)/shard_map/convert_element_type | solution.py:215
  (3 shorter events, 0.0 us)
Async XLA Ops:
  0.0 89.6 %copy-start = (bf16[6,192]{1,0:T(8,128)(2,1)S(1)}, bf16[6,192]{1,0:T(8,128)(2,1)}, u32[]{:S(2)}) copy-start(bf16[6,192]{1,0:T(8,128)(2,1)} %param.9) | copy-start | bytes 6916
  1.8 35.0 %collective-permute-start.2 = (bf16[1152,3072]{1,0:T(8,128)(2,1)}, bf16[1152,3072]{1,0:T(8,128)(2,1)}, u32[]{:S(2)}, u32[]{:S(2)}) collective-permute-start(bf16[1152,3072]{1,0:T(8,128)(2,1)} %bitcast.10), channel_id=1, source_target_pairs={{0,1},{1,0},{2,3},{3,2},{4,5},{5,4},{6,7},{7,6},{8,9},{9,8},{10,11... | collective-permute-start | bytes 21233672 | tf_op jit(solution)/shard_map/ppermute | solution.py:166
  5.1 18.3 %collective-permute-start = (bf16[512,3072]{1,0:T(8,128)(2,1)}, bf16[512,3072]{1,0:T(8,128)(2,1)}, u32[]{:S(2)}, u32[]{:S(2)}) collective-permute-start(bf16[512,3072]{1,0:T(8,128)(2,1)} %alphas_ref.1), channel_id=1, source_target_pairs={{0,1},{1,0},{2,3},{3,2},{4,5},{5,4},{6,7},{7,6},{8,9},{9,8},{10,11... | collective-permute-start | bytes 9437192 | tf_op jit(solution)/shard_map/ppermute | solution.py:160
  5.2 18.2 %collective-permute-start.1 = (bf16[288,3072]{1,0:T(8,128)(2,1)}, bf16[288,3072]{1,0:T(8,128)(2,1)}, u32[]{:S(2)}, u32[]{:S(2)}) collective-permute-start(bf16[288,3072]{1,0:T(8,128)(2,1)} %bitcast.13), channel_id=1, source_target_pairs={{0,1},{1,0},{2,3},{3,2},{4,5},{5,4},{6,7},{7,6},{8,9},{9,8},{10,11... | collective-permute-start | bytes 5308424 | tf_op jit(solution)/shard_map/ppermute | solution.py:160
  6.3 30.5 %all-to-all-start = ((s32[64,8,128]{2,1,0:T(8,128)}), s32[64,8,128]{2,1,0:T(8,128)S(1)}, u32[]{:S(2)}, u32[]{:S(2)}) async-start(s32[64,8,128]{2,1,0:T(8,128)} %tile.2), calls=%async_computation | async-start | bytes 524288 | tf_op jit(solution)/shard_map/all_to_all | solution.py:167
  36.9 0.7 copy-start.1
  88.3 5.8 %collective-permute-start.3 = (bf16[192,256]{1,0:T(8,128)(2,1)}, bf16[192,256]{1,0:T(8,128)(2,1)S(1)}, u32[]{:S(2)}, u32[]{:S(2)}) collective-permute-start(bf16[192,256]{1,0:T(8,128)(2,1)} %get-tuple-element.12), channel_id=1, source_target_pairs={{0,2},{2,0},{1,3},{3,1},{4,6},{6,4},{5,7},{7,5},{8,10},{10,8},{9,1... | collective-permute-start | bytes 294920 | tf_op jit(solution)/shard_map/ppermute | solution.py:211

commit v4 on v3

v4 whole, which is shorter than its diff:
```python
import jax
import jax.numpy as jnp
from jax import lax
from jax.experimental import pallas as pl
from jax.experimental.pallas import tpu as pltpu
from jax.sharding import Mesh
from jax.sharding import PartitionSpec as P

S = 12288
ACTS = 6
OBS = 48
ALPHAS = 512
BELIEFS = 1024
BEL = ("z", "x", "yl")
PEERS = 64
OWN = BELIEFS // PEERS
COLS = 3072
ROWS = 192
HALF = COLS // 128
LINES = 2 * HALF
PITCH = 64
GAP = 56
PART = 256
WEIGHTS = ALPHAS * PITCH
TOTAL = WEIGHTS + ACTS * OBS * LINES
STAGE = 32
DISCOUNT = 0.95

NT = (((1,), (1,)), ((), ()))


def choose_kernel(index_ref, action_ref, out_ref, row_ref):
    bel = (lax.axis_index("z") * 4 + lax.axis_index("x")) * 2 + lax.axis_index("yl")
    row_ref[...] = jnp.zeros_like(row_ref)
    for r in range(OWN):
        row_ref[r : r + 1, :OBS] = index_ref[action_ref[bel * OWN + r], r : r + 1, :]
    packed = row_ref[:8] + pltpu.roll(row_ref[8:], 64, axis=1)
    out_ref[...] = jnp.broadcast_to(packed[None], (PEERS, 8, 128))


def prep_kernel(alphas_ref, alphas2_ref, observe_ref, observe2_ref, lines_ref, stage_ref, wide_ref, out_ref, sems, out_sems):
    def spread(sources, steps, first, pitch):
        def copies(t, slot):
            return [
                pltpu.make_async_copy(
                    source.at[pl.ds(pl.multiple_of(t * STAGE, STAGE), STAGE), :], stage_ref.at[slot, s], sems.at[slot, s]
                )
                for s, source in enumerate(sources)
            ]

        def result(t, slot):
            at = pl.multiple_of(first + t * STAGE * pitch, 16)
            return pltpu.make_async_copy(
                out_ref.at[slot, pl.ds(0, STAGE * pitch), :], lines_ref.at[pl.ds(at, STAGE * pitch), :], out_sems.at[slot]
            )

        for slot in range(3):
            for copy in copies(slot, slot):
                copy.start()

        def step(t, _):
            slot = lax.rem(t, 4)
            side = lax.rem(t, 2)

            @pl.when(t + 3 < steps)
            def _():
                for copy in copies(t + 3, lax.rem(t + 3, 4)):
                    copy.start()

            for copy in copies(t, slot):
                copy.wait()

            @pl.when(t >= 2)
            def _():
                result(t - 2, side).wait()

            for g in range(STAGE // 16):
                for s in range(2):
                    for j in range(HALF):
                        part = stage_ref[slot, s, g * 16 : (g + 1) * 16, j * 128 : (j + 1) * 128]
                        wide_ref[g, pl.ds(s * HALF + j, 16, stride=GAP), :] = part.astype(jnp.float32)
                for r in range(16):
                    at = (g * 16 + r) * pitch
                    out_ref[side, at : at + LINES, :] = wide_ref[g, r * GAP : r * GAP + LINES, :].astype(jnp.bfloat16)
            result(t, side).start()
            return 0

        lax.fori_loop(0, steps, step, 0)
        for t in (steps - 2, steps - 1):
            result(t, t % 2).wait()

    spread((alphas_ref, alphas2_ref), ALPHAS // STAGE, 0, PITCH)
    spread((observe_ref, observe2_ref), ACTS * OBS // STAGE, WEIGHTS, LINES)


def pick(owner, got):
    value = got[:ROWS]
    for a in range(1, ACTS):
        value = jnp.where(owner == a, got[a * ROWS : (a + 1) * ROWS], value)
    return value


def main_kernel(
    index_ref, action_ref, owner_ref, source_ref, here_ref, there_ref,
    send_ref, mixed_ref, lines_ref, index_smem, weights_ref, mix_ref, block_ref, weight_sems, index_sem, lines_sem, mixed_sem,
):
    fetch = [
        pltpu.make_async_copy(source, weights_ref.at[n], weight_sems.at[n])
        for n, source in enumerate((here_ref, there_ref))
    ]
    lines = pltpu.make_async_copy(source_ref, lines_ref, lines_sem)
    table = pltpu.make_async_copy(index_ref, index_smem, index_sem)
    lines.start()
    table.start()
    for copy in fetch:
        copy.start()
    table.wait()
    lines.wait()
    rows_ref = lines_ref.at[pl.ds(0, WEIGHTS), :].reshape(ALPHAS, PITCH, 128)
    obs_ref = lines_ref.at[pl.ds(WEIGHTS, ACTS * OBS * LINES), :].reshape(ACTS * OBS, LINES, 128)
    high = lax.axis_index("yh")
    core = lax.axis_index("co")

    def sixteen(n, _):
        t = n // 16
        i = lax.rem(n, 16)
        source = (2 * jnp.where(t == 0, 1 - high, high) + core) * 16 + i
        for h in range(2):
            for r in range(8):
                a = action_ref[source * 16 + h * 8 + r]
                own = index_smem.at[source, r]
                weight = obs_ref.at[pl.ds(a * OBS, OBS)]
                total = None
                for o in range(OBS):
                    term = rows_ref[own[h * 64 + o], :LINES, :].astype(jnp.float32) * weight[o].astype(jnp.float32)
                    total = term if o == 0 else total + term
                mix_ref[(h * 8 + r) * GAP : (h * 8 + r) * GAP + LINES, :] = total
        for j in range(LINES):
            part = mix_ref[pl.ds(j, 16, stride=GAP), :]
            at = pl.ds(pl.multiple_of(i * 16, 16), 16)
            block_ref[t, j // HALF, at, (j % HALF) * 128 : (j % HALF + 1) * 128] = part.astype(jnp.bfloat16)
        return 0

    lax.fori_loop(0, 2 * PART // 16, sixteen, 0)
    mixed = pltpu.make_async_copy(block_ref.at[1], mixed_ref, mixed_sem)
    mixed.start()
    for copy in fetch:
        copy.wait()
    got = lax.dot_general(weights_ref[0], block_ref[0, 0], NT, preferred_element_type=jnp.float32)
    got += lax.dot_general(weights_ref[1], block_ref[0, 1], NT, preferred_element_type=jnp.float32)
    first = pl.multiple_of((2 * (1 - high) + core) * PART, 128)
    send_ref[...] = pick(owner_ref[:, pl.ds(first, PART)], got).astype(send_ref.dtype)
    mixed.wait()


def rest_kernel(owner_ref, mixed_ref, here_ref, there_ref, keep_ref, sum_ref):
    step = pl.program_id(0)
    got = lax.dot_general(here_ref[...], mixed_ref[0], NT, preferred_element_type=jnp.float32)
    got += lax.dot_general(there_ref[...], mixed_ref[1], NT, preferred_element_type=jnp.float32)

    @pl.when(step == 0)
    def _():
        sum_ref[...] = got

    @pl.when(step > 0)
    def _():
        sum_ref[...] += got

    @pl.when(step == pl.num_programs(0) - 1)
    def _():
        first = pl.multiple_of((2 * lax.axis_index("yh") + lax.axis_index("co")) * PART, 128)
        keep_ref[...] = pick(owner_ref[:, pl.ds(first, PART)], sum_ref[...])


def vmem():
    return pl.BlockSpec(memory_space=pltpu.VMEM)


def smem():
    return pl.BlockSpec(memory_space=pltpu.SMEM)


def hbm():
    return pl.BlockSpec(memory_space=pltpu.HBM)


def gather_blocks(packed):
    return lax.all_to_all(packed, BEL, 0, 0, tiled=True)


def body(alphas, transitions, observe, reward, belief_index, action):
    core = lax.axis_index("co")
    high = lax.axis_index("yh")
    across = [(0, 1), (1, 0)]
    observe = observe.reshape(ACTS * OBS, COLS)
    transitions = transitions.reshape(ACTS * ROWS, COLS)
    alphas2 = lax.ppermute(alphas, "co", across)
    observe2 = lax.ppermute(observe, "co", across)
    packed = pl.pallas_call(
        choose_kernel,
        out_shape=jax.ShapeDtypeStruct((PEERS, 8, 128), jnp.int32),
        in_specs=[vmem(), smem()],
        out_specs=vmem(),
        scratch_shapes=[pltpu.VMEM((OWN, 128), jnp.int32)],
        name="choose",
    )(belief_index.transpose(1, 0, 2), action)
    index = gather_blocks(packed)
    transitions2 = lax.ppermute(transitions, "co", across)
    lines = pl.pallas_call(
        prep_kernel,
        out_shape=jax.ShapeDtypeStruct((TOTAL, 128), jnp.bfloat16),
        in_specs=[hbm()] * 4,
        out_specs=hbm(),
        scratch_shapes=[
            pltpu.VMEM((4, 2, STAGE, COLS), jnp.bfloat16),
            pltpu.VMEM((STAGE // 16, 16 * GAP, 128), jnp.float32),
            pltpu.VMEM((2, STAGE * PITCH, 128), jnp.bfloat16),
            pltpu.SemaphoreType.DMA((4, 2)),
            pltpu.SemaphoreType.DMA((2,)),
        ],
        compiler_params=pltpu.CompilerParams(vmem_limit_bytes=62 * 2**20),
        cost_estimate=pl.CostEstimate(flops=8 * 10**9, bytes_accessed=10**7, transcendentals=0),
        name="prep",
    )(alphas, alphas2, observe, observe2)
    owner = action.reshape(1, BELIEFS)
    send, mixed = pl.pallas_call(
        main_kernel,
        out_shape=(
            jax.ShapeDtypeStruct((ROWS, PART), jnp.bfloat16),
            jax.ShapeDtypeStruct((2, PART, COLS), jnp.bfloat16),
        ),
        in_specs=[vmem(), smem(), vmem(), hbm(), hbm(), hbm()],
        out_specs=(vmem(), hbm()),
        scratch_shapes=[
            pltpu.VMEM((TOTAL, 128), jnp.bfloat16),
            pltpu.SMEM((PEERS, 8, 128), jnp.int32),
            pltpu.VMEM((2, ACTS * ROWS, COLS), jnp.bfloat16),
            pltpu.VMEM((16 * GAP, 128), jnp.float32),
            pltpu.VMEM((2, 2, PART, COLS), jnp.bfloat16),
            pltpu.SemaphoreType.DMA((2,)),
            pltpu.SemaphoreType.DMA,
            pltpu.SemaphoreType.DMA,
            pltpu.SemaphoreType.DMA,
        ],
        compiler_params=pltpu.CompilerParams(vmem_limit_bytes=62 * 2**20),
        name="mix",
    )(index, action, owner, lines, transitions, transitions2)
    got = lax.ppermute(send, "yh", across)
    wide = 512
    keep = pl.pallas_call(
        rest_kernel,
        grid=(COLS // wide,),
        out_shape=jax.ShapeDtypeStruct((ROWS, PART), jnp.float32),
        in_specs=[
            pl.BlockSpec((1, BELIEFS), lambda t: (0, 0)),
            pl.BlockSpec((2, PART, wide), lambda t: (0, 0, t)),
            pl.BlockSpec((ACTS * ROWS, wide), lambda t: (0, t)),
            pl.BlockSpec((ACTS * ROWS, wide), lambda t: (0, t)),
        ],
        out_specs=pl.BlockSpec((ROWS, PART), lambda t: (0, 0)),
        scratch_shapes=[pltpu.VMEM((ACTS * ROWS, PART), jnp.float32)],
        compiler_params=pltpu.CompilerParams(vmem_limit_bytes=62 * 2**20),
        cost_estimate=pl.CostEstimate(flops=4 * 10**9, bytes_accessed=17 * 10**6, transcendentals=0),
        name="rest",
    )(owner, mixed, transitions, transitions2)
    summed = keep + got.astype(jnp.float32)
    row_action = lax.dynamic_slice_in_dim(action, (2 * high + core) * PART, PART)
    picked = (row_action[:, None] == jnp.arange(ACTS, dtype=jnp.int32)[None, :]).astype(jnp.bfloat16)
    gained = jnp.dot(picked, reward, preferred_element_type=jnp.float32)
    return (gained + DISCOUNT / S * summed.T).astype(jnp.bfloat16)


def solution(mesh):
    torus = Mesh(mesh.devices.reshape(8, 4, 2, 2, 2), ("z", "x", "yl", "yh", "co"))
    st = ("yh", "co")
    in_specs = (
        P(None, st),
        P(None, BEL, st),
        P(None, None, st),
        P(None, BEL),
        P(BEL, None, None),
        P(),
    )
    return jax.shard_map(body, mesh=torus, in_specs=in_specs, out_specs=P(st, BEL), check_vma=False)
```

time: 96.1 us -> 98.2 us (1.022)
  Pallas kernels: 64.2 us -> 74.1 us
  waiting for transfers between devices: 8.84 us -> 4.07 us
  other arithmetic: 3.23 us -> 1.61 us
  local copies, waits for them, and re-layouts: 3.04 us -> 1.46 us
    pallas_call x0 -> x2, Pallas kernels: none -> 12 us  [the longest x1 10.3 us: body(): pl.pallas_call(rest_kernel, grid=(COLS // wide,), out_shape=jax.ShapeDtyp...]
    ppermute x4, waiting for transfers between devices: 8.84 us -> 4.06 us  [the longest x1 4.06 us: body(): observe2 = lax.ppermute(observe, 'co', across)]
    pallas_call x1, Pallas kernels: 50.7 us -> 47.5 us  [body(): pl.pallas_call(main_kernel, out_shape=(jax.ShapeDtypeStruct((ROWS, PART),...]
    pallas_call x1, Pallas kernels: 13.5 us -> 14.6 us  [body(): pl.pallas_call(prep_kernel, out_shape=jax.ShapeDtypeStruct((TOTAL, 128),...]
  transfers between devices with their start and end apart: 5 -> 5, of which waited for: 2 -> 1; matrix products, arithmetic and copies ran while one was open for 3% -> 1% of each run, Pallas kernels for 14% -> 27%
where the time goes in v4:
time: 98.2 us; the launch traced here: 97.5 us
  Pallas kernels  74.1 us (75%)
  starting transfers between devices  16 us (16%)
  waiting for transfers between devices  4.07 us (4%)
  other arithmetic  1.61 us (2%)
  local copies, waits for them, and re-layouts  1.46 us (1%)
    pallas_call x1, Pallas kernels, body(): pl.pallas_call(main_kernel, out_shape=(jax.ShapeDtypeStruct((ROWS, PART),...  47.5 us
    pallas_call x1, Pallas kernels, body(): pl.pallas_call(prep_kernel, out_shape=jax.ShapeDtypeStruct((TOTAL, 128),...  14.6 us
    all_to_all x1, starting transfers between devices, gather_blocks(): return lax.all_to_all(packed, BEL, 0, 0, tiled=True)  11 us
    pallas_call x1, Pallas kernels, body(): pl.pallas_call(rest_kernel, grid=(COLS // wide,), out_shape=jax.ShapeDtyp...  10.3 us
    ppermute x1, waiting for transfers between devices, body(): observe2 = lax.ppermute(observe, 'co', across)  4.06 us
    ppermute x1, starting transfers between devices, body(): transitions2 = lax.ppermute(transitions, 'co', across)  3.2 us
  transfers between devices with their start and end apart: 5, of which 1 were waited for; matrix products, arithmetic and copies ran while one was open for 1% of the time, Pallas kernels for 27%

profile of v4, /device:TPU:1, one launch (start us, length us, event | category | flops | bytes accessed | tf_op | source)
XLA Modules:
  0.0 97.5 jit_solution(10963692813776167150)
XLA Ops:
  0.0 0.0 copy-start
  0.0 3.2 %collective-permute-start.2 = (bf16[1152,3072]{1,0:T(8,128)(2,1)}, bf16[1152,3072]{1,0:T(8,128)(2,1)}, u32[]{:S(2)}, u32[]{:S(2)}) collective-permute-start(bf16[1152,3072]{1,0:T(8,128)(2,1)} %bitcast.9), channel_id=1, source_target_pairs={{0,1},{1,0},{2,3},{3,2},{4,5},{5,4},{6,7},{7,6},{8,9},{9,8},{10,11... | collective-permute-start | bytes 21233672 | tf_op jit(solution)/shard_map/ppermute | solution.py:208
  3.2 0.0 collective-permute-start
  3.2 0.5 collective-permute-start.1
  3.7 1.7 %choose.1 = s32[64,8,128]{2,1,0:T(8,128)} custom-call(s32[6,16,48]{2,1,0:T(8,128)} %bitcast.14, s32[1024]{0:T(1024)} %action_ref.3), custom_call_target="tpu_custom_call" | custom-call | tf_op jit(solution)/shard_map/choose/pallas_call | solution.py:199
  5.4 11.0 %all-to-all-start = ((s32[64,8,128]{2,1,0:T(8,128)}), s32[64,8,128]{2,1,0:T(8,128)S(1)}, u32[]{:S(2)}, u32[]{:S(2)}) async-start(s32[64,8,128]{2,1,0:T(8,128)} %choose.1), calls=%async_computation | async-start | bytes 524288 | tf_op jit(solution)/shard_map/all_to_all | solution.py:188
  16.4 0.8 dynamic_slice.3
  17.1 0.0 copy-done
  17.1 0.3 fusion.1
  17.4 4.1 %collective-permute-done.1.observe2_ref = bf16[288,3072]{1,0:T(8,128)(2,1)} collective-permute-done((bf16[288,3072]{1,0:T(8,128)(2,1)}, bf16[288,3072]{1,0:T(8,128)(2,1)}, u32[]{:S(2)}, u32[]{:S(2)}) %collective-permute-start.1) | collective-permute-done | bytes 1769504 | tf_op jit(solution)/shard_map/ppermute | solution.py:198
  21.5 0.0 collective-permute-done.alphas2_ref
  21.5 14.6 %prep.1.source_ref = bf16[46592,128]{1,0:T(8,128)(2,1)} custom-call(bf16[512,3072]{1,0:T(8,128)(2,1)} %alphas_ref.1, bf16[512,3072]{1,0:T(8,128)(2,1)} %collective-permute-done.alphas2_ref, bf16[288,3072]{1,0:T(8,128)(2,1)} %bitcast.16, bf16[288,3072]{1,0:T(8,128)(2,1)} %collective-permute-done.1.observe2_ref), custom_call_target="tpu_custom_call" | custom-call | flops 8000000000 | bytes 10000000 | tf_op jit(solution)/shard_map/prep/pallas_call | solution.py:209
  36.0 0.0 all-to-all-done.index_ref
  36.1 0.0 copy-start.1
  36.1 0.0 collective-permute-done.2.there_ref
  36.1 0.7 copy-done.1
  36.8 47.5 %mix.1 = (bf16[192,256]{1,0:T(8,128)(2,1)}, bf16[2,256,3072]{2,1,0:T(8,128)(2,1)}) custom-call(s32[64,8,128]{2,1,0:T(8,128)} %copy-done.1, s32[1024]{0:T(1024)} %action_ref.3, s32[1,1024]{1,0:T(1,128)} %bitcast.12, bf16[46592,128]{1,0:T(8,128)(2,1)} %prep.1.source_ref, bf16[1152,3072]{1,0:T(8,128)(2,1)} %bitcast.10, ...), custom_call_target="tpu_custom_call" | custom-call | tf_op jit(solution)/shard_map/mix/pallas_call | solution.py:226
  84.3 1.3 %collective-permute-start.3 = (bf16[192,256]{1,0:T(8,128)(2,1)}, bf16[192,256]{1,0:T(8,128)(2,1)S(1)}, u32[]{:S(2)}, u32[]{:S(2)}) collective-permute-start(bf16[192,256]{1,0:T(8,128)(2,1)} %get-tuple-element.8), channel_id=1, source_target_pairs={{0,2},{2,0},{1,3},{3,1},{4,6},{6,4},{5,7},{7,5},{8,10},{10,8},{9,1... | collective-permute-start | bytes 294920 | tf_op jit(solution)/shard_map/ppermute | solution.py:248
  85.6 10.3 %rest.1 = f32[192,256]{1,0:T(8,128)} custom-call(s32[1,1024]{1,0:T(1,128)} %bitcast.13, bf16[2,256,3072]{2,1,0:T(8,128)(2,1)} %get-tuple-element.7.mixed_ref, bf16[1152,3072]{1,0:T(8,128)(2,1)} %bitcast.11, bf16[1152,3072]{1,0:T(8,128)(2,1)} %collective-permute-done.2.there_ref), custom_call_target="tpu_custom_call" | custom-call | flops 4000000000 | bytes 17000000 | tf_op jit(solution)/shard_map/rest/pallas_call | solution.py:250
  95.9 0.0 collective-permute-done.3
  95.9 1.6 %fusion = bf16[256,192]{0,1:T(8,128)(2,1)} fusion(f32[256,192]{0,1:T(8,128)S(1)} %fusion.1, f32[192,256]{1,0:T(8,128)} %rest.1, bf16[192,256]{1,0:T(8,128)(2,1)S(1)} %collective-permute-done.3), kind=kLoop, calls=%fused_computation.1 | loop fusion | flops 245760 | bytes 589824 | tf_op jit(solution)/shard_map/convert_element_type | solution.py:270
Async XLA Ops:
  0.0 17.1 %copy-start = (bf16[6,192]{1,0:T(8,128)(2,1)S(1)}, bf16[6,192]{1,0:T(8,128)(2,1)}, u32[]{:S(2)}) copy-start(bf16[6,192]{1,0:T(8,128)(2,1)} %param.9) | copy-start | bytes 6916
  0.0 36.1 %collective-permute-start.2 = (bf16[1152,3072]{1,0:T(8,128)(2,1)}, bf16[1152,3072]{1,0:T(8,128)(2,1)}, u32[]{:S(2)}, u32[]{:S(2)}) collective-permute-start(bf16[1152,3072]{1,0:T(8,128)(2,1)} %bitcast.9), channel_id=1, source_target_pairs={{0,1},{1,0},{2,3},{3,2},{4,5},{5,4},{6,7},{7,6},{8,9},{9,8},{10,11... | collective-permute-start | bytes 21233672 | tf_op jit(solution)/shard_map/ppermute | solution.py:208
  3.2 18.3 %collective-permute-start = (bf16[512,3072]{1,0:T(8,128)(2,1)}, bf16[512,3072]{1,0:T(8,128)(2,1)}, u32[]{:S(2)}, u32[]{:S(2)}) collective-permute-start(bf16[512,3072]{1,0:T(8,128)(2,1)} %alphas_ref.1), channel_id=1, source_target_pairs={{0,1},{1,0},{2,3},{3,2},{4,5},{5,4},{6,7},{7,6},{8,9},{9,8},{10,11... | collective-permute-start | bytes 9437192 | tf_op jit(solution)/shard_map/ppermute | solution.py:197
  3.2 18.3 %collective-permute-start.1 = (bf16[288,3072]{1,0:T(8,128)(2,1)}, bf16[288,3072]{1,0:T(8,128)(2,1)}, u32[]{:S(2)}, u32[]{:S(2)}) collective-permute-start(bf16[288,3072]{1,0:T(8,128)(2,1)} %bitcast.15), channel_id=1, source_target_pairs={{0,1},{1,0},{2,3},{3,2},{4,5},{5,4},{6,7},{7,6},{8,9},{9,8},{10,11... | collective-permute-start | bytes 5308424 | tf_op jit(solution)/shard_map/ppermute | solution.py:198
  5.4 30.6 %all-to-all-start = ((s32[64,8,128]{2,1,0:T(8,128)}), s32[64,8,128]{2,1,0:T(8,128)S(1)}, u32[]{:S(2)}, u32[]{:S(2)}) async-start(s32[64,8,128]{2,1,0:T(8,128)} %choose.1), calls=%async_computation | async-start | bytes 524288 | tf_op jit(solution)/shard_map/all_to_all | solution.py:188
  36.1 0.7 copy-start.1
  84.3 11.6 %collective-permute-start.3 = (bf16[192,256]{1,0:T(8,128)(2,1)}, bf16[192,256]{1,0:T(8,128)(2,1)S(1)}, u32[]{:S(2)}, u32[]{:S(2)}) collective-permute-start(bf16[192,256]{1,0:T(8,128)(2,1)} %get-tuple-element.8), channel_id=1, source_target_pairs={{0,2},{2,0},{1,3},{3,1},{4,6},{6,4},{5,7},{7,5},{8,10},{10,8},{9,1... | collective-permute-start | bytes 294920 | tf_op jit(solution)/shard_map/ppermute | solution.py:248

commit v5 on v4

v5 whole, which is shorter than its diff:
```python
import jax
import jax.numpy as jnp
from jax import lax
from jax.experimental import pallas as pl
from jax.experimental.pallas import tpu as pltpu
from jax.sharding import Mesh
from jax.sharding import PartitionSpec as P

S = 12288
ACTS = 6
OBS = 48
ALPHAS = 512
BELIEFS = 1024
BEL = ("z", "x", "yl")
PEERS = 64
OWN = BELIEFS // PEERS
COLS = 3072
ROWS = 192
HALF = COLS // 128
LINES = 2 * HALF
PITCH = 64
GAP = 56
PART = 256
WEIGHTS = ALPHAS * PITCH
TOTAL = WEIGHTS + ACTS * OBS * LINES
STAGE = 32
DISCOUNT = 0.95

NT = (((1,), (1,)), ((), ()))


def choose_kernel(index_ref, action_ref, out_ref, row_ref):
    bel = (lax.axis_index("z") * 4 + lax.axis_index("x")) * 2 + lax.axis_index("yl")
    row_ref[...] = jnp.zeros_like(row_ref)
    for r in range(OWN):
        row_ref[r : r + 1, :OBS] = index_ref[action_ref[bel * OWN + r], r : r + 1, :]
    packed = row_ref[:8] + pltpu.roll(row_ref[8:], 64, axis=1)
    out_ref[...] = jnp.broadcast_to(packed[None], (PEERS, 8, 128))


def prep_kernel(
    alphas_ref, alphas2_ref, observe_ref, observe2_ref, lines_ref, rows_in, obs_in, wide_ref, out_ref, in_sems, out_sems
):
    parts = (
        ((alphas_ref, alphas2_ref), rows_in, ALPHAS // STAGE, 0, 0, PITCH),
        ((observe_ref, observe2_ref), obs_in, ACTS * OBS // STAGE, ALPHAS // STAGE, WEIGHTS, LINES),
    )

    def copy_in(part, t, s):
        sources, dest, _, at, _, _ = part
        here = pl.ds(pl.multiple_of(t * STAGE, STAGE), STAGE)
        return pltpu.make_async_copy(sources[s].at[here, :], dest.at[s, here, :], in_sems.at[at + t, s])

    def copy_out(part, t):
        _, _, _, at, first, pitch = part
        here = pl.ds(pl.multiple_of(first + t * STAGE * pitch, 16), STAGE * pitch)
        return pltpu.make_async_copy(out_ref.at[here, :], lines_ref.at[here, :], out_sems.at[at + t])

    for part in parts:

        def begin(t, _, part=part):
            for s in range(2):
                copy_in(part, t, s).start()
            return 0

        lax.fori_loop(0, part[2], begin, 0)
    for part in parts:

        def step(t, _, part=part):
            _, staged, _, _, first, pitch = part
            for s in range(2):
                copy_in(part, t, s).wait()
            for g in range(STAGE // 16):
                here = pl.ds(pl.multiple_of(t * STAGE + g * 16, 16), 16)
                for s in range(2):
                    for j in range(HALF):
                        got = staged[s, here, j * 128 : (j + 1) * 128]
                        wide_ref[g, pl.ds(s * HALF + j, 16, stride=GAP), :] = got.astype(jnp.float32)
                for r in range(16):
                    at = pl.multiple_of(first + (t * STAGE + g * 16 + r) * pitch, 16)
                    out_ref[pl.ds(at, LINES), :] = wide_ref[g, r * GAP : r * GAP + LINES, :].astype(jnp.bfloat16)
            copy_out(part, t).start()
            return 0

        lax.fori_loop(0, part[2], step, 0)
    for part in parts:

        def finish(t, _, part=part):
            copy_out(part, t).wait()
            return 0

        lax.fori_loop(0, part[2], finish, 0)


def pick(owner, got):
    value = got[:ROWS]
    for a in range(1, ACTS):
        value = jnp.where(owner == a, got[a * ROWS : (a + 1) * ROWS], value)
    return value


def main_kernel(
    index_ref, action_ref, owner_ref, source_ref, here_ref, there_ref,
    send_ref, mixed_ref, mixed2_ref, lines_ref, index_smem, weights_ref, mix_ref, block_ref, weight_sems, index_sem, lines_sem, mixed_sem,
):
    fetch = [
        pltpu.make_async_copy(source, weights_ref.at[n], weight_sems.at[n])
        for n, source in enumerate((here_ref, there_ref))
    ]
    lines = pltpu.make_async_copy(source_ref, lines_ref, lines_sem)
    table = pltpu.make_async_copy(index_ref, index_smem, index_sem)
    lines.start()
    table.start()
    for copy in fetch:
        copy.start()
    table.wait()
    lines.wait()
    rows_ref = lines_ref.at[pl.ds(0, WEIGHTS), :].reshape(ALPHAS, PITCH, 128)
    obs_ref = lines_ref.at[pl.ds(WEIGHTS, ACTS * OBS * LINES), :].reshape(ACTS * OBS, LINES, 128)
    high = lax.axis_index("yh")
    core = lax.axis_index("co")

    def sixteen(n, _):
        t = n // 16
        i = lax.rem(n, 16)
        source = (2 * jnp.where(t == 0, 1 - high, high) + core) * 16 + i
        for h in range(2):
            for r in range(8):
                a = action_ref[source * 16 + h * 8 + r]
                own = index_smem.at[source, r]
                weight = obs_ref.at[pl.ds(a * OBS, OBS)]
                total = None
                for o in range(OBS):
                    term = rows_ref[own[h * 64 + o], :LINES, :].astype(jnp.float32) * weight[o].astype(jnp.float32)
                    total = term if o == 0 else total + term
                mix_ref[(h * 8 + r) * GAP : (h * 8 + r) * GAP + LINES, :] = total
        for j in range(LINES):
            part = mix_ref[pl.ds(j, 16, stride=GAP), :]
            at = pl.ds(pl.multiple_of(i * 16, 16), 16)
            block_ref[t, j // HALF, at, (j % HALF) * 128 : (j % HALF + 1) * 128] = part.astype(jnp.bfloat16)
        return 0

    lax.fori_loop(0, 2 * PART // 16, sixteen, 0)
    mixed = [
        pltpu.make_async_copy(block_ref.at[1, n], out, mixed_sem.at[n]) for n, out in enumerate((mixed_ref, mixed2_ref))
    ]
    for copy in mixed:
        copy.start()
    for copy in fetch:
        copy.wait()
    got = lax.dot_general(weights_ref[0], block_ref[0, 0], NT, preferred_element_type=jnp.float32)
    got += lax.dot_general(weights_ref[1], block_ref[0, 1], NT, preferred_element_type=jnp.float32)
    first = pl.multiple_of((2 * (1 - high) + core) * PART, 128)
    send_ref[...] = pick(owner_ref[:, pl.ds(first, PART)], got).astype(send_ref.dtype)
    for copy in mixed:
        copy.wait()


def vmem():
    return pl.BlockSpec(memory_space=pltpu.VMEM)


def smem():
    return pl.BlockSpec(memory_space=pltpu.SMEM)


def hbm():
    return pl.BlockSpec(memory_space=pltpu.HBM)


def gather_blocks(packed):
    return lax.all_to_all(packed, BEL, 0, 0, tiled=True)


def body(alphas, transitions, observe, reward, belief_index, action):
    core = lax.axis_index("co")
    high = lax.axis_index("yh")
    across = [(0, 1), (1, 0)]
    observe = observe.reshape(ACTS * OBS, COLS)
    transitions = transitions.reshape(ACTS * ROWS, COLS)
    alphas2 = lax.ppermute(alphas, "co", across)
    observe2 = lax.ppermute(observe, "co", across)
    packed = pl.pallas_call(
        choose_kernel,
        out_shape=jax.ShapeDtypeStruct((PEERS, 8, 128), jnp.int32),
        in_specs=[vmem(), smem()],
        out_specs=vmem(),
        scratch_shapes=[pltpu.VMEM((OWN, 128), jnp.int32)],
        name="choose",
    )(belief_index.transpose(1, 0, 2), action)
    index = gather_blocks(packed)
    transitions2 = lax.ppermute(transitions, "co", across)
    lines = pl.pallas_call(
        prep_kernel,
        out_shape=jax.ShapeDtypeStruct((TOTAL, 128), jnp.bfloat16),
        in_specs=[hbm()] * 4,
        out_specs=hbm(),
        scratch_shapes=[
            pltpu.VMEM((2, ALPHAS, COLS), jnp.bfloat16),
            pltpu.VMEM((2, ACTS * OBS, COLS), jnp.bfloat16),
            pltpu.VMEM((STAGE // 16, 16 * GAP, 128), jnp.float32),
            pltpu.VMEM((TOTAL, 128), jnp.bfloat16),
            pltpu.SemaphoreType.DMA(((ALPHAS + ACTS * OBS) // STAGE, 2)),
            pltpu.SemaphoreType.DMA(((ALPHAS + ACTS * OBS) // STAGE,)),
        ],
        compiler_params=pltpu.CompilerParams(vmem_limit_bytes=62 * 2**20),
        cost_estimate=pl.CostEstimate(flops=8 * 10**9, bytes_accessed=10**7, transcendentals=0),
        name="prep",
    )(alphas, alphas2, observe, observe2)
    owner = action.reshape(1, BELIEFS)
    send, mixed, mixed2 = pl.pallas_call(
        main_kernel,
        out_shape=(
            jax.ShapeDtypeStruct((ROWS, PART), jnp.bfloat16),
            jax.ShapeDtypeStruct((PART, COLS), jnp.bfloat16),
            jax.ShapeDtypeStruct((PART, COLS), jnp.bfloat16),
        ),
        in_specs=[vmem(), smem(), vmem(), hbm(), hbm(), hbm()],
        out_specs=(vmem(), hbm(), hbm()),
        scratch_shapes=[
            pltpu.VMEM((TOTAL, 128), jnp.bfloat16),
            pltpu.SMEM((PEERS, 8, 128), jnp.int32),
            pltpu.VMEM((2, ACTS * ROWS, COLS), jnp.bfloat16),
            pltpu.VMEM((16 * GAP, 128), jnp.float32),
            pltpu.VMEM((2, 2, PART, COLS), jnp.bfloat16),
            pltpu.SemaphoreType.DMA((2,)),
            pltpu.SemaphoreType.DMA,
            pltpu.SemaphoreType.DMA,
            pltpu.SemaphoreType.DMA((2,)),
        ],
        compiler_params=pltpu.CompilerParams(vmem_limit_bytes=62 * 2**20),
        name="mix",
    )(index, action, owner, lines, transitions, transitions2)
    got = lax.ppermute(send, "yh", across)
    carried = lax.dot_general(transitions, mixed, NT, preferred_element_type=jnp.float32)
    carried += lax.dot_general(transitions2, mixed2, NT, preferred_element_type=jnp.float32)
    summed = pick(lax.dynamic_slice_in_dim(owner, (2 * high + core) * PART, PART, 1), carried) + got.astype(jnp.float32)
    row_action = lax.dynamic_slice_in_dim(action, (2 * high + core) * PART, PART)
    picked = (row_action[:, None] == jnp.arange(ACTS, dtype=jnp.int32)[None, :]).astype(jnp.bfloat16)
    gained = jnp.dot(picked, reward, preferred_element_type=jnp.float32)
    return (gained + DISCOUNT / S * summed.T).astype(jnp.bfloat16)


def solution(mesh):
    torus = Mesh(mesh.devices.reshape(8, 4, 2, 2, 2), ("z", "x", "yl", "yh", "co"))
    st = ("yh", "co")
    in_specs = (
        P(None, st),
        P(None, BEL, st),
        P(None, None, st),
        P(None, BEL),
        P(BEL, None, None),
        P(),
    )
    return jax.shard_map(body, mesh=torus, in_specs=in_specs, out_specs=P(st, BEL), check_vma=False)
```

time: 98.2 us -> 91.7 us (0.934)
  Pallas kernels: 74.1 us -> 57.9 us
  matrix products: 0.27 us -> 11.1 us
    dot_general x0 -> x2, matrix products: none -> 10.8 us  [the longest x1 5.67 us: body(): lax.dot_general(transitions2, mixed2, NT, preferred_element_type=jnp.floa...]
    pallas_call x1 -> x0, Pallas kernels: 10.3 us -> none  [body(): pl.pallas_call(rest_kernel, grid=(COLS // wide,), out_shape=jax.ShapeDtyp...]
    pallas_call x1, Pallas kernels: 14.6 us -> 8.73 us  [body(): pl.pallas_call(prep_kernel, out_shape=jax.ShapeDtypeStruct((TOTAL, 128),...]
  transfers between devices with their start and end apart: 5 -> 5, of which waited for: 1 -> 1; matrix products, arithmetic and copies ran while one was open for 1% -> 13% of each run, Pallas kernels for 27% -> 11%
where the time goes in v5:
time: 91.7 us; the launch traced here: 91.4 us
  Pallas kernels  57.9 us (63%)
  starting transfers between devices  16 us (17%)
  matrix products  11.1 us (12%)
  waiting for transfers between devices  4.06 us (4%)
  other arithmetic  1.51 us (2%)
    pallas_call x1, Pallas kernels, body(): pl.pallas_call(main_kernel, out_shape=(jax.ShapeDtypeStruct((ROWS, PART),...  47.5 us
    all_to_all x1, starting transfers between devices, gather_blocks(): return lax.all_to_all(packed, BEL, 0, 0, tiled=True)  11 us
    pallas_call x1, Pallas kernels, body(): pl.pallas_call(prep_kernel, out_shape=jax.ShapeDtypeStruct((TOTAL, 128),...  8.73 us
    dot_general x1, matrix products, body(): lax.dot_general(transitions2, mixed2, NT, preferred_element_type=jnp.floa...  5.67 us
    dot_general x1, matrix products, body(): lax.dot_general(transitions, mixed, NT, preferred_element_type=jnp.float32)  5.15 us
    ppermute x1, waiting for transfers between devices, body(): observe2 = lax.ppermute(observe, 'co', across)  4.05 us
    ppermute x1, starting transfers between devices, body(): transitions2 = lax.ppermute(transitions, 'co', across)  3.2 us
  transfers between devices with their start and end apart: 5, of which 1 were waited for; matrix products, arithmetic and copies ran while one was open for 13% of the time, Pallas kernels for 11%

profile of v5, /device:TPU:1, one launch (start us, length us, event | category | flops | bytes accessed | tf_op | source)
XLA Modules:
  0.0 91.4 jit_solution(8899210202231608768)
XLA Ops:
  0.0 0.0 copy-start
  0.0 3.2 %collective-permute-start.2 = (bf16[1152,3072]{1,0:T(8,128)(2,1)}, bf16[1152,3072]{1,0:T(8,128)(2,1)}, u32[]{:S(2)}, u32[]{:S(2)}) collective-permute-start(bf16[1152,3072]{1,0:T(8,128)(2,1)} %bitcast.17), channel_id=1, source_target_pairs={{0,1},{1,0},{2,3},{3,2},{4,5},{5,4},{6,7},{7,6},{8,9},{9,8},{10,11... | collective-permute-start | bytes 21233672 | tf_op jit(solution)/shard_map/ppermute | solution.py:192
  3.2 0.0 collective-permute-start
  3.2 0.5 collective-permute-start.1
  3.7 1.7 %choose.1 = s32[64,8,128]{2,1,0:T(8,128)} custom-call(s32[6,16,48]{2,1,0:T(8,128)} %bitcast.20, s32[1024]{0:T(1024)} %action_ref.3), custom_call_target="tpu_custom_call" | custom-call | tf_op jit(solution)/shard_map/choose/pallas_call | solution.py:183
  5.4 11.0 %all-to-all-start = ((s32[64,8,128]{2,1,0:T(8,128)}), s32[64,8,128]{2,1,0:T(8,128)S(1)}, u32[]{:S(2)}, u32[]{:S(2)}) async-start(s32[64,8,128]{2,1,0:T(8,128)} %choose.1), calls=%async_computation | async-start | bytes 524288 | tf_op jit(solution)/shard_map/all_to_all | solution.py:172
  16.4 0.8 broadcast_compare_fusion.4
  17.1 0.0 copy-done
  17.2 0.3 fusion.10
  17.4 4.1 %collective-permute-done.1.observe2_ref = bf16[288,3072]{1,0:T(8,128)(2,1)} collective-permute-done((bf16[288,3072]{1,0:T(8,128)(2,1)}, bf16[288,3072]{1,0:T(8,128)(2,1)}, u32[]{:S(2)}, u32[]{:S(2)}) %collective-permute-start.1) | collective-permute-done | bytes 1769504 | tf_op jit(solution)/shard_map/ppermute | solution.py:182
  21.5 0.0 collective-permute-done.alphas2_ref
  21.5 8.7 %prep.1.source_ref = bf16[46592,128]{1,0:T(8,128)(2,1)} custom-call(bf16[512,3072]{1,0:T(8,128)(2,1)} %alphas_ref.1, bf16[512,3072]{1,0:T(8,128)(2,1)} %collective-permute-done.alphas2_ref, bf16[288,3072]{1,0:T(8,128)(2,1)} %bitcast.23, bf16[288,3072]{1,0:T(8,128)(2,1)} %collective-permute-done.1.observe2_ref), custom_call_target="tpu_custom_call" | custom-call | flops 8000000000 | bytes 10000000 | tf_op jit(solution)/shard_map/prep/pallas_call | solution.py:193
  30.2 0.0 all-to-all-done.index_ref
  30.2 0.0 copy-start.1
  30.2 0.0 collective-permute-done.2.there_ref
  30.3 0.7 copy-done.1
  31.0 47.5 %mix.1 = (bf16[192,256]{1,0:T(8,128)(2,1)}, bf16[256,3072]{1,0:T(8,128)(2,1)}, bf16[256,3072]{1,0:T(8,128)(2,1)}) custom-call(s32[64,8,128]{2,1,0:T(8,128)} %copy-done.1, s32[1024]{0:T(1024)} %action_ref.3, s32[1,1024]{1,0:T(1,128)} %bitcast.21, bf16[46592,128]{1,0:T(8,128)(2,1)} %prep.1.source_ref, bf16[1152,3072]{1,0:T(8,128)(2,1)} %bitcast.18, ...), custom_call_target="tpu_custom_call" | custom-call | tf_op jit(solution)/shard_map/mix/pallas_call | solution.py:211
  78.5 1.3 %collective-permute-start.3 = (bf16[192,256]{1,0:T(8,128)(2,1)}, bf16[192,256]{1,0:T(8,128)(2,1)S(1)}, u32[]{:S(2)}, u32[]{:S(2)}) collective-permute-start(bf16[192,256]{1,0:T(8,128)(2,1)} %get-tuple-element.10), channel_id=1, source_target_pairs={{0,2},{2,0},{1,3},{3,1},{4,6},{6,4},{5,7},{7,5},{8,10},{10,8},{9,1... | collective-permute-start | bytes 294920 | tf_op jit(solution)/shard_map/ppermute | solution.py:234
  79.8 0.0 copy-start.2
  79.8 5.7 %fusion.12 = f32[256,1152]{0,1:T(8,128)S(1)} fusion(bf16[256,3072]{1,0:T(8,128)(2,1)} %get-tuple-element.9, bf16[1152,3072]{1,0:T(8,128)(2,1)} %collective-permute-done.2.there_ref), kind=kOutput, calls=%fused_computation.20 | convolution fusion | flops 1811939328 | bytes 9830400 | tf_op jit(solution)/shard_map/dot_general | solution.py:236
  85.5 0.0 copy-done.2
  85.5 5.1 %fusion = f32[1152,256]{1,0:T(8,128)S(1)} fusion(f32[256,1152]{0,1:T(8,128)S(1)} %fusion.12, bf16[256,3072]{1,0:T(8,128)(2,1)S(1)} %copy-done.2, bf16[1152,3072]{1,0:T(8,128)(2,1)} %bitcast.19), kind=kOutput, calls=%fused_computation.1 | convolution fusion | flops 1812234240 | bytes 11010048 | tf_op jit(solution)/shard_map/dot_general | solution.py:235
  90.6 0.0 collective-permute-done.3
  90.6 0.7 fusion.9
  (1 shorter events, 0.0 us)
Async XLA Ops:
  0.0 17.1 %copy-start = (bf16[6,192]{1,0:T(8,128)(2,1)S(1)}, bf16[6,192]{1,0:T(8,128)(2,1)}, u32[]{:S(2)}) copy-start(bf16[6,192]{1,0:T(8,128)(2,1)} %param.9) | copy-start | bytes 6916
  0.0 30.2 %collective-permute-start.2 = (bf16[1152,3072]{1,0:T(8,128)(2,1)}, bf16[1152,3072]{1,0:T(8,128)(2,1)}, u32[]{:S(2)}, u32[]{:S(2)}) collective-permute-start(bf16[1152,3072]{1,0:T(8,128)(2,1)} %bitcast.17), channel_id=1, source_target_pairs={{0,1},{1,0},{2,3},{3,2},{4,5},{5,4},{6,7},{7,6},{8,9},{9,8},{10,11... | collective-permute-start | bytes 21233672 | tf_op jit(solution)/shard_map/ppermute | solution.py:192
  3.2 18.3 %collective-permute-start = (bf16[512,3072]{1,0:T(8,128)(2,1)}, bf16[512,3072]{1,0:T(8,128)(2,1)}, u32[]{:S(2)}, u32[]{:S(2)}) collective-permute-start(bf16[512,3072]{1,0:T(8,128)(2,1)} %alphas_ref.1), channel_id=1, source_target_pairs={{0,1},{1,0},{2,3},{3,2},{4,5},{5,4},{6,7},{7,6},{8,9},{9,8},{10,11... | collective-permute-start | bytes 9437192 | tf_op jit(solution)/shard_map/ppermute | solution.py:181
  3.2 18.3 %collective-permute-start.1 = (bf16[288,3072]{1,0:T(8,128)(2,1)}, bf16[288,3072]{1,0:T(8,128)(2,1)}, u32[]{:S(2)}, u32[]{:S(2)}) collective-permute-start(bf16[288,3072]{1,0:T(8,128)(2,1)} %bitcast.22), channel_id=1, source_target_pairs={{0,1},{1,0},{2,3},{3,2},{4,5},{5,4},{6,7},{7,6},{8,9},{9,8},{10,11... | collective-permute-start | bytes 5308424 | tf_op jit(solution)/shard_map/ppermute | solution.py:182
  5.4 24.8 %all-to-all-start = ((s32[64,8,128]{2,1,0:T(8,128)}), s32[64,8,128]{2,1,0:T(8,128)S(1)}, u32[]{:S(2)}, u32[]{:S(2)}) async-start(s32[64,8,128]{2,1,0:T(8,128)} %choose.1), calls=%async_computation | async-start | bytes 524288 | tf_op jit(solution)/shard_map/all_to_all | solution.py:172
  30.2 0.7 copy-start.1
  78.5 12.1 %collective-permute-start.3 = (bf16[192,256]{1,0:T(8,128)(2,1)}, bf16[192,256]{1,0:T(8,128)(2,1)S(1)}, u32[]{:S(2)}, u32[]{:S(2)}) collective-permute-start(bf16[192,256]{1,0:T(8,128)(2,1)} %get-tuple-element.10), channel_id=1, source_target_pairs={{0,2},{2,0},{1,3},{3,1},{4,6},{6,4},{5,7},{7,5},{8,10},{10,8},{9,1... | collective-permute-start | bytes 294920 | tf_op jit(solution)/shard_map/ppermute | solution.py:234
  79.8 5.7 %copy-start.2 = (bf16[256,3072]{1,0:T(8,128)(2,1)S(1)}, bf16[256,3072]{1,0:T(8,128)(2,1)}, u32[]{:S(2)}) copy-start(bf16[256,3072]{1,0:T(8,128)(2,1)} %get-tuple-element.8) | copy-start | bytes 4718596

commit v6 on v5

--- a/solution.py
+++ b/solution.py
@@ -20,6 +20,7 @@
 LINES = 2 * HALF
 PITCH = 64
 GAP = 56
+ODD = 49
 PART = 256
 WEIGHTS = ALPHAS * PITCH
 TOTAL = WEIGHTS + ACTS * OBS * LINES
@@ -101,24 +102,29 @@
 
 def main_kernel(
     index_ref, action_ref, owner_ref, source_ref, here_ref, there_ref,
-    send_ref, mixed_ref, mixed2_ref, lines_ref, index_smem, weights_ref, mix_ref, block_ref, weight_sems, index_sem, lines_sem, mixed_sem,
+    send_ref, keep_ref, lines_ref, index_smem, weights_ref, mix_ref, block_ref, weight_sems, index_sems, lines_sem,
 ):
     fetch = [
         pltpu.make_async_copy(source, weights_ref.at[n], weight_sems.at[n])
         for n, source in enumerate((here_ref, there_ref))
     ]
     lines = pltpu.make_async_copy(source_ref, lines_ref, lines_sem)
-    table = pltpu.make_async_copy(index_ref, index_smem, index_sem)
+    high = lax.axis_index("yh")
+    core = lax.axis_index("co")
+    tables = []
+    for t, yh in enumerate((1 - high, high)):
+        source = pl.ds((2 * yh + core) * 16, 16)
+        tables.append(pltpu.make_async_copy(index_ref.at[source], index_smem.at[source], index_sems.at[t]))
+    tables[0].start()
     lines.start()
-    table.start()
+    tables[1].start()
     for copy in fetch:
         copy.start()
-    table.wait()
+    for copy in tables:
+        copy.wait()
     lines.wait()
     rows_ref = lines_ref.at[pl.ds(0, WEIGHTS), :].reshape(ALPHAS, PITCH, 128)
     obs_ref = lines_ref.at[pl.ds(WEIGHTS, ACTS * OBS * LINES), :].reshape(ACTS * OBS, LINES, 128)
-    high = lax.axis_index("yh")
-    core = lax.axis_index("co")
 
     def sixteen(n, _):
         t = n // 16
@@ -127,33 +133,39 @@
         for h in range(2):
             for r in range(8):
                 a = action_ref[source * 16 + h * 8 + r]
-                own = index_smem.at[source, r]
                 weight = obs_ref.at[pl.ds(a * OBS, OBS)]
                 total = None
                 for o in range(OBS):
-                    term = rows_ref[own[h * 64 + o], :LINES, :].astype(jnp.float32) * weight[o].astype(jnp.float32)
+                    term = rows_ref[index_smem[source, r, h * 64 + o], :LINES, :].astype(jnp.float32) * weight[o].astype(jnp.float32)
                     total = term if o == 0 else total + term
-                mix_ref[(h * 8 + r) * GAP : (h * 8 + r) * GAP + LINES, :] = total
+                mix_ref[(h * 8 + r) * ODD : (h * 8 + r) * ODD + LINES, :] = total
         for j in range(LINES):
-            part = mix_ref[pl.ds(j, 16, stride=GAP), :]
+            part = mix_ref[pl.ds(j, 16, stride=ODD), :]
             at = pl.ds(pl.multiple_of(i * 16, 16), 16)
             block_ref[t, j // HALF, at, (j % HALF) * 128 : (j % HALF + 1) * 128] = part.astype(jnp.bfloat16)
         return 0
 
     lax.fori_loop(0, 2 * PART // 16, sixteen, 0)
-    mixed = [
-        pltpu.make_async_copy(block_ref.at[1, n], out, mixed_sem.at[n]) for n, out in enumerate((mixed_ref, mixed2_ref))
-    ]
-    for copy in mixed:
-        copy.start()
     for copy in fetch:
         copy.wait()
-    got = lax.dot_general(weights_ref[0], block_ref[0, 0], NT, preferred_element_type=jnp.float32)
-    got += lax.dot_general(weights_ref[1], block_ref[0, 1], NT, preferred_element_type=jnp.float32)
-    first = pl.multiple_of((2 * (1 - high) + core) * PART, 128)
-    send_ref[...] = pick(owner_ref[:, pl.ds(first, PART)], got).astype(send_ref.dtype)
-    for copy in mixed:
-        copy.wait()
+
+    def product(t, _):
+        got = lax.dot_general(weights_ref[0], block_ref[t, 0], NT, preferred_element_type=jnp.float32)
+        got += lax.dot_general(weights_ref[1], block_ref[t, 1], NT, preferred_element_type=jnp.float32)
+        first = pl.multiple_of((2 * jnp.where(t == 0, 1 - high, high) + core) * PART, 128)
+        value = pick(owner_ref[:, pl.ds(first, PART)], got)
+
+        @pl.when(t == 0)
+        def _():
+            send_ref[...] = value.astype(send_ref.dtype)
+
+        @pl.when(t == 1)
+        def _():
+            keep_ref[...] = value
+
+        return 0
+
+    lax.fori_loop(0, 2, product, 0)
 
 
 def vmem():
@@ -208,33 +220,29 @@
         name="prep",
     )(alphas, alphas2, observe, observe2)
     owner = action.reshape(1, BELIEFS)
-    send, mixed, mixed2 = pl.pallas_call(
+    send, keep = pl.pallas_call(
         main_kernel,
         out_shape=(
             jax.ShapeDtypeStruct((ROWS, PART), jnp.bfloat16),
-            jax.ShapeDtypeStruct((PART, COLS), jnp.bfloat16),
-            jax.ShapeDtypeStruct((PART, COLS), jnp.bfloat16),
+            jax.ShapeDtypeStruct((ROWS, PART), jnp.float32),
         ),
-        in_specs=[vmem(), smem(), vmem(), hbm(), hbm(), hbm()],
-        out_specs=(vmem(), hbm(), hbm()),
+        in_specs=[hbm(), smem(), vmem(), hbm(), hbm(), hbm()],
+        out_specs=(vmem(), vmem()),
         scratch_shapes=[
             pltpu.VMEM((TOTAL, 128), jnp.bfloat16),
             pltpu.SMEM((PEERS, 8, 128), jnp.int32),
             pltpu.VMEM((2, ACTS * ROWS, COLS), jnp.bfloat16),
-            pltpu.VMEM((16 * GAP, 128), jnp.float32),
+            pltpu.VMEM((16 * ODD, 128), jnp.float32),
             pltpu.VMEM((2, 2, PART, COLS), jnp.bfloat16),
             pltpu.SemaphoreType.DMA((2,)),
+            pltpu.SemaphoreType.DMA((2,)),
             pltpu.SemaphoreType.DMA,
-            pltpu.SemaphoreType.DMA,
-            pltpu.SemaphoreType.DMA((2,)),
         ],
         compiler_params=pltpu.CompilerParams(vmem_limit_bytes=62 * 2**20),
         name="mix",
     )(index, action, owner, lines, transitions, transitions2)
     got = lax.ppermute(send, "yh", across)
-    carried = lax.dot_general(transitions, mixed, NT, preferred_element_type=jnp.float32)
-    carried += lax.dot_general(transitions2, mixed2, NT, preferred_element_type=jnp.float32)
-    summed = pick(lax.dynamic_slice_in_dim(owner, (2 * high + core) * PART, PART, 1), carried) + got.astype(jnp.float32)
+    summed = keep + got.astype(jnp.float32)
     row_action = lax.dynamic_slice_in_dim(action, (2 * high + core) * PART, PART)
     picked = (row_action[:, None] == jnp.arange(ACTS, dtype=jnp.int32)[None, :]).astype(jnp.bfloat16)
     gained = jnp.dot(picked, reward, preferred_element_type=jnp.float32)

time: 91.7 us -> 88.3 us (0.963)
  matrix products: 11.1 us -> 0.27 us
  waiting for transfers between devices: 4.06 us -> 8.55 us
  Pallas kernels: 57.9 us -> 60.1 us
    dot_general x2 -> x0, matrix products: 10.8 us -> none  [the longest x1 5.67 us: body(): lax.dot_general(transitions2, mixed2, NT, preferred_element_type=jnp.floa...]
    ppermute x1, waiting for transfers between devices: 0.01 us -> 4.2 us  [body(): got = lax.ppermute(send, 'yh', across)]
    pallas_call x1, Pallas kernels: 47.5 us -> 49.7 us  [body(): pl.pallas_call(main_kernel, out_shape=(jax.ShapeDtypeStruct((ROWS, PART),...]
  transfers between devices with their start and end apart: 5 -> 5, of which waited for: 1 -> 2; matrix products, arithmetic and copies ran while one was open for 13% -> 1% of each run, Pallas kernels for 11% -> 12%
where the time goes in v6:
time: 88.3 us; the launch traced here: 88 us
  Pallas kernels  60.1 us (68%)
  starting transfers between devices  16 us (18%)
  waiting for transfers between devices  8.55 us (10%)
  other arithmetic  1.6 us (2%)
  local copies, waits for them, and re-layouts  1.47 us (2%)
    pallas_call x1, Pallas kernels, body(): pl.pallas_call(main_kernel, out_shape=(jax.ShapeDtypeStruct((ROWS, PART),...  49.7 us
    all_to_all x1, starting transfers between devices, gather_blocks(): return lax.all_to_all(packed, BEL, 0, 0, tiled=True)  11 us
    pallas_call x1, Pallas kernels, body(): pl.pallas_call(prep_kernel, out_shape=jax.ShapeDtypeStruct((TOTAL, 128),...  8.73 us
    ppermute x1, waiting for transfers between devices, body(): observe2 = lax.ppermute(observe, 'co', across)  4.34 us
    ppermute x1, waiting for transfers between devices, body(): got = lax.ppermute(send, 'yh', across)  4.2 us
    ppermute x1, starting transfers between devices, body(): transitions2 = lax.ppermute(transitions, 'co', across)  3.2 us
  transfers between devices with their start and end apart: 5, of which 2 were waited for; matrix products, arithmetic and copies ran while one was open for 1% of the time, Pallas kernels for 12%

profile of v6, /device:TPU:1, one launch (start us, length us, event | category | flops | bytes accessed | tf_op | source)
XLA Modules:
  0.0 88.0 jit_solution(4656731037024903594)
XLA Ops:
  0.0 0.0 copy-start
  0.0 3.2 %collective-permute-start.2 = (bf16[1152,3072]{1,0:T(8,128)(2,1)}, bf16[1152,3072]{1,0:T(8,128)(2,1)}, u32[]{:S(2)}, u32[]{:S(2)}) collective-permute-start(bf16[1152,3072]{1,0:T(8,128)(2,1)} %bitcast.9), channel_id=1, source_target_pairs={{0,1},{1,0},{2,3},{3,2},{4,5},{5,4},{6,7},{7,6},{8,9},{9,8},{10,11... | collective-permute-start | bytes 21233672 | tf_op jit(solution)/shard_map/ppermute | solution.py:204
  3.2 0.0 collective-permute-start
  3.2 0.5 collective-permute-start.1
  3.7 1.7 %choose.1 = s32[64,8,128]{2,1,0:T(8,128)} custom-call(s32[6,16,48]{2,1,0:T(8,128)} %bitcast.11, s32[1024]{0:T(1024)} %action_ref.3), custom_call_target="tpu_custom_call" | custom-call | tf_op jit(solution)/shard_map/choose/pallas_call | solution.py:195
  5.4 11.0 %all-to-all-start = ((s32[64,8,128]{2,1,0:T(8,128)}), s32[64,8,128]{2,1,0:T(8,128)S(1)}, u32[]{:S(2)}, u32[]{:S(2)}) async-start(s32[64,8,128]{2,1,0:T(8,128)} %choose.1), calls=%async_computation | async-start | bytes 524288 | tf_op jit(solution)/shard_map/all_to_all | solution.py:184
  16.4 0.8 dynamic_slice.3
  17.1 4.3 %collective-permute-done.1.observe2_ref = bf16[288,3072]{1,0:T(8,128)(2,1)} collective-permute-done((bf16[288,3072]{1,0:T(8,128)(2,1)}, bf16[288,3072]{1,0:T(8,128)(2,1)}, u32[]{:S(2)}, u32[]{:S(2)}) %collective-permute-start.1) | collective-permute-done | bytes 1769504 | tf_op jit(solution)/shard_map/ppermute | solution.py:194
  21.5 0.0 collective-permute-done.alphas2_ref
  21.5 8.7 %prep.1.source_ref = bf16[46592,128]{1,0:T(8,128)(2,1)} custom-call(bf16[512,3072]{1,0:T(8,128)(2,1)} %alphas_ref.1, bf16[512,3072]{1,0:T(8,128)(2,1)} %collective-permute-done.alphas2_ref, bf16[288,3072]{1,0:T(8,128)(2,1)} %bitcast.14, bf16[288,3072]{1,0:T(8,128)(2,1)} %collective-permute-done.1.observe2_ref), custom_call_target="tpu_custom_call" | custom-call | flops 8000000000 | bytes 10000000 | tf_op jit(solution)/shard_map/prep/pallas_call | solution.py:205
  30.2 0.0 all-to-all-done.index_ref
  30.2 0.0 copy-start.1
  30.3 0.0 collective-permute-done.2.there_ref
  30.3 0.7 copy-done.1
  31.0 49.7 %mix.1 = (bf16[192,256]{1,0:T(8,128)(2,1)}, f32[192,256]{1,0:T(8,128)}) custom-call(s32[64,8,128]{2,1,0:T(8,128)} %copy-done.1, s32[1024]{0:T(1024)} %action_ref.3, s32[1,1024]{1,0:T(1,128)} %bitcast.12, bf16[46592,128]{1,0:T(8,128)(2,1)} %prep.1.source_ref, bf16[1152,3072]{1,0:T(8,128)(2,1)} %bitcast.10, bf16[1152,3072]{1,0:T(8,128)(2,1)} %collective-permute-done.2.there_ref), custom_call_target="tpu_custom_call" | custom-call | tf_op jit(solution)/shard_map/mix/pallas_call | solution.py:223
  80.6 1.3 %collective-permute-start.3 = (bf16[192,256]{1,0:T(8,128)(2,1)}, bf16[192,256]{1,0:T(8,128)(2,1)S(1)}, u32[]{:S(2)}, u32[]{:S(2)}) collective-permute-start(bf16[192,256]{1,0:T(8,128)(2,1)} %get-tuple-element.8), channel_id=1, source_target_pairs={{0,2},{2,0},{1,3},{3,1},{4,6},{6,4},{5,7},{7,5},{8,10},{10,8},{9,1... | collective-permute-start | bytes 294920 | tf_op jit(solution)/shard_map/ppermute | solution.py:244
  81.9 0.0 copy-done
  81.9 0.3 fusion.1
  82.2 4.2 %collective-permute-done.3 = bf16[192,256]{1,0:T(8,128)(2,1)S(1)} collective-permute-done((bf16[192,256]{1,0:T(8,128)(2,1)}, bf16[192,256]{1,0:T(8,128)(2,1)S(1)}, u32[]{:S(2)}, u32[]{:S(2)}) %collective-permute-start.3) | collective-permute-done | bytes 98336 | tf_op jit(solution)/shard_map/ppermute | solution.py:244
  86.4 1.6 %fusion = bf16[256,192]{0,1:T(8,128)(2,1)} fusion(f32[256,192]{0,1:T(8,128)S(1)} %fusion.1, f32[192,256]{1,0:T(8,128)} %get-tuple-element.7, bf16[192,256]{1,0:T(8,128)(2,1)S(1)} %collective-permute-done.3), kind=kLoop, calls=%fused_computation.1 | loop fusion | flops 245760 | bytes 589824 | tf_op jit(solution)/shard_map/convert_element_type | solution.py:249
Async XLA Ops:
  0.0 81.9 %copy-start = (bf16[6,192]{1,0:T(8,128)(2,1)S(1)}, bf16[6,192]{1,0:T(8,128)(2,1)}, u32[]{:S(2)}) copy-start(bf16[6,192]{1,0:T(8,128)(2,1)} %param.9) | copy-start | bytes 6916
  0.0 30.3 %collective-permute-start.2 = (bf16[1152,3072]{1,0:T(8,128)(2,1)}, bf16[1152,3072]{1,0:T(8,128)(2,1)}, u32[]{:S(2)}, u32[]{:S(2)}) collective-permute-start(bf16[1152,3072]{1,0:T(8,128)(2,1)} %bitcast.9), channel_id=1, source_target_pairs={{0,1},{1,0},{2,3},{3,2},{4,5},{5,4},{6,7},{7,6},{8,9},{9,8},{10,11... | collective-permute-start | bytes 21233672 | tf_op jit(solution)/shard_map/ppermute | solution.py:204
  3.2 18.3 %collective-permute-start = (bf16[512,3072]{1,0:T(8,128)(2,1)}, bf16[512,3072]{1,0:T(8,128)(2,1)}, u32[]{:S(2)}, u32[]{:S(2)}) collective-permute-start(bf16[512,3072]{1,0:T(8,128)(2,1)} %alphas_ref.1), channel_id=1, source_target_pairs={{0,1},{1,0},{2,3},{3,2},{4,5},{5,4},{6,7},{7,6},{8,9},{9,8},{10,11... | collective-permute-start | bytes 9437192 | tf_op jit(solution)/shard_map/ppermute | solution.py:193
  3.2 18.3 %collective-permute-start.1 = (bf16[288,3072]{1,0:T(8,128)(2,1)}, bf16[288,3072]{1,0:T(8,128)(2,1)}, u32[]{:S(2)}, u32[]{:S(2)}) collective-permute-start(bf16[288,3072]{1,0:T(8,128)(2,1)} %bitcast.13), channel_id=1, source_target_pairs={{0,1},{1,0},{2,3},{3,2},{4,5},{5,4},{6,7},{7,6},{8,9},{9,8},{10,11... | collective-permute-start | bytes 5308424 | tf_op jit(solution)/shard_map/ppermute | solution.py:194
  5.4 24.8 %all-to-all-start = ((s32[64,8,128]{2,1,0:T(8,128)}), s32[64,8,128]{2,1,0:T(8,128)S(1)}, u32[]{:S(2)}, u32[]{:S(2)}) async-start(s32[64,8,128]{2,1,0:T(8,128)} %choose.1), calls=%async_computation | async-start | bytes 524288 | tf_op jit(solution)/shard_map/all_to_all | solution.py:184
  30.2 0.7 copy-start.1
  80.6 5.8 %collective-permute-start.3 = (bf16[192,256]{1,0:T(8,128)(2,1)}, bf16[192,256]{1,0:T(8,128)(2,1)S(1)}, u32[]{:S(2)}, u32[]{:S(2)}) collective-permute-start(bf16[192,256]{1,0:T(8,128)(2,1)} %get-tuple-element.8), channel_id=1, source_target_pairs={{0,2},{2,0},{1,3},{3,1},{4,6},{6,4},{5,7},{7,5},{8,10},{10,8},{9,1... | collective-permute-start | bytes 294920 | tf_op jit(solution)/shard_map/ppermute | solution.py:244
